TPU v7x, 256 devices: a whole 4x4x8 slice. The times are simulated.
256 devices in a mesh: seq: 32 (over x, y, core), head: 8 (over z).
Axes of the slice: x: 4, y: 4, z: 8, core: 2. Of those that a mesh axis runs over, the one named last changes fastest.
Arguments:
- query_rows: bfloat16 [32768, 4096], P(('seq', 'head')), may hold values from -1.796875 to 1.796875
- key_rows: bfloat16 [32768, 4096], P(('seq', 'head')), may hold values from -1.796875 to 1.796875
- value_rows: bfloat16 [32768, 4096], P(('seq', 'head')), may hold values from -1.796875 to 1.796875
- out_grad: bfloat16 [32768, 4096], P(('seq', 'head')), may hold values from -1.796875 to 1.796875
- decay: float32 [32, 32768], P('head', 'seq'), may hold values from 0 to 2
Outputs:
- attended: bfloat16 [32768, 4096], P(('seq', 'head'))
- query_grad: bfloat16 [32768, 4096], P(('seq', 'head'))
- key_grad: bfloat16 [32768, 4096], P(('seq', 'head'))
- value_grad: bfloat16 [32768, 4096], P(('seq', 'head'))
All inputs are finite; a program needn't handle non-finite values.
Results may differ from a plain program's by a relative error of at most 0.0083.
Values may be sent and summed in bfloat16 or wider, within the bound.
A program may use at most 128 MiB of HBM per device.

v0:
```python
import jax
import jax.numpy as jnp
from jax import lax
from jax.sharding import PartitionSpec as P


def copy_for_each(x, axis):
    size = lax.axis_size(axis)
    return lax.all_to_all(jnp.broadcast_to(x[None], (size, *x.shape)), axis, 0, 0, tiled=True)


def joined_along(pieces, dim):
    pieces = jnp.moveaxis(pieces, 0, dim)
    lengths = pieces.shape
    return pieces.reshape(*lengths[:dim], lengths[dim] * lengths[dim + 1], *lengths[dim + 2 :])


def gathered_copies(x, axis, dim):
    pieces = copy_for_each(x, axis)
    return joined_along(pieces, dim)


def on_device(query_rows, key_rows, value_rows, out_grad, decay):
    query_local, key_local, value_local, grad_local = (
        lax.all_to_all(query_rows, "head", split_axis=1, concat_axis=0, tiled=True),
        lax.all_to_all(key_rows, "head", split_axis=1, concat_axis=0, tiled=True),
        lax.all_to_all(value_rows, "head", split_axis=1, concat_axis=0, tiled=True),
        lax.all_to_all(out_grad, "head", split_axis=1, concat_axis=0, tiled=True),
    )
    heads_here = decay.shape[0]
    width = query_local.shape[1] // heads_here
    scale_factor = width ** (-0.5)
    running = jnp.cumsum(decay, axis=1)
    block_log = running[:, -1]
    weights = jnp.exp(-(block_log[:, None] - running))
    growth = jnp.exp(-running)
    length = decay.shape[1]
    causal = jnp.arange(length)[:, None] >= jnp.arange(length)[None, :]
    head_data = []
    local_parts = []
    updates = []
    sources = []
    for member in range(heads_here):
        query_head = query_local[:, member * width : (member + 1) * width]
        key_head = key_local[:, member * width : (member + 1) * width]
        value_head = value_local[:, member * width : (member + 1) * width]
        grad_head = grad_local[:, member * width : (member + 1) * width]
        spread_log = running[member][:, None] - running[member][None, :]
        decay_mask = jnp.where(causal, jnp.exp(-jnp.where(causal, spread_log, 0.0)), 0.0)
        scores = (
            scale_factor
            * jnp.dot(query_head, key_head.T, preferred_element_type=jnp.float32)
            * decay_mask
        ).astype(jnp.bfloat16)
        grad_scores = (
            scale_factor
            * jnp.dot(grad_head, value_head.T, preferred_element_type=jnp.float32)
            * decay_mask
        ).astype(jnp.bfloat16)
        attended_part = jnp.dot(scores, value_head, preferred_element_type=jnp.float32)
        query_part = jnp.dot(grad_scores, key_head, preferred_element_type=jnp.float32)
        key_part = jnp.dot(grad_scores.T, query_head, preferred_element_type=jnp.float32)
        value_part = jnp.dot(scores.T, grad_head, preferred_element_type=jnp.float32)
        keyed = (key_head * weights[member][:, None]).astype(jnp.bfloat16)
        queried = (query_head * growth[member][:, None]).astype(jnp.bfloat16)
        updates.append(jnp.dot(keyed.T, value_head, preferred_element_type=jnp.float32))
        sources.append(
            scale_factor * jnp.dot(queried.T, grad_head, preferred_element_type=jnp.float32)
        )
        head_data.append((query_head, key_head, value_head, grad_head))
        local_parts.append((attended_part, query_part, key_part, value_part))
    update_stack = jnp.stack(updates)
    source_stack = jnp.stack(sources)
    zero_state = jnp.zeros_like(update_stack)
    all_logs = gathered_copies(block_log[None], "seq", 0)
    position = lax.axis_index("seq")
    block_ends = jnp.cumsum(all_logs, axis=0)
    own_end = lax.dynamic_index_in_dim(block_ends, position, 0, keepdims=False)
    own_start = own_end - block_log
    update_piece = lax.all_gather(
        update_stack[None].astype(jnp.bfloat16), "seq", axis=0, tiled=True
    ).astype(jnp.float32)
    source_piece = lax.all_gather(
        source_stack[None].astype(jnp.bfloat16), "seq", axis=0, tiled=True
    ).astype(jnp.float32)
    rows_here = update_piece.shape[0]
    block_index = jnp.arange(rows_here)
    before = (block_index < position)[:, None]
    after = (block_index > position)[:, None]
    forward_weight = jnp.where(
        before, jnp.exp(-jnp.where(before, own_start[None] - block_ends, 0.0)), 0.0
    )
    backward_weight = jnp.where(
        after, jnp.exp(-jnp.where(after, block_ends - all_logs - own_end[None], 0.0)), 0.0
    )
    forward_sum = jnp.sum(forward_weight[:, :, None, None] * update_piece, axis=0)
    backward_sum = jnp.sum(backward_weight[:, :, None, None] * source_piece, axis=0)
    state_in = zero_state + forward_sum
    state_grad = zero_state + backward_sum
    state_half = state_in.astype(jnp.bfloat16)
    grad_half = state_grad.astype(jnp.bfloat16)
    attended_list = []
    query_list = []
    key_list = []
    value_list = []
    for member in range(heads_here):
        query_head, key_head, value_head, grad_head = head_data[member]
        attended_part, query_part, key_part, value_part = local_parts[member]
        growth_col = growth[member][:, None]
        weight_col = weights[member][:, None]
        attended_list.append(
            (
                attended_part
                + scale_factor
                * growth_col
                * jnp.dot(query_head, state_half[member], preferred_element_type=jnp.float32)
            ).astype(jnp.bfloat16)
        )
        query_list.append(
            (
                query_part
                + scale_factor
                * growth_col
                * jnp.dot(grad_head, state_half[member].T, preferred_element_type=jnp.float32)
            ).astype(jnp.bfloat16)
        )
        key_list.append(
            (
                key_part
                + weight_col
                * jnp.dot(value_head, grad_half[member].T, preferred_element_type=jnp.float32)
            ).astype(jnp.bfloat16)
        )
        value_list.append(
            (
                value_part
                + weight_col
                * jnp.dot(key_head, grad_half[member], preferred_element_type=jnp.float32)
            ).astype(jnp.bfloat16)
        )
    attended = jnp.concatenate(attended_list, axis=1)
    query_grad = jnp.concatenate(query_list, axis=1)
    key_grad = jnp.concatenate(key_list, axis=1)
    value_grad = jnp.concatenate(value_list, axis=1)
    attended_out, query_out, key_out, value_out = (
        lax.all_to_all(attended, "head", split_axis=0, concat_axis=1, tiled=True),
        lax.all_to_all(query_grad, "head", split_axis=0, concat_axis=1, tiled=True),
        lax.all_to_all(key_grad, "head", split_axis=0, concat_axis=1, tiled=True),
        lax.all_to_all(value_grad, "head", split_axis=0, concat_axis=1, tiled=True),
    )
    return (attended_out, query_out, key_out, value_out)


def solution(mesh):
    in_specs = (
        P(("seq", "head"), None),
        P(("seq", "head"), None),
        P(("seq", "head"), None),
        P(("seq", "head"), None),
        P("head", "seq"),
    )
    out_specs = (
        P(("seq", "head"), None),
        P(("seq", "head"), None),
        P(("seq", "head"), None),
        P(("seq", "head"), None),
    )
    return jax.shard_map(
        on_device, mesh=mesh, in_specs=in_specs, out_specs=out_specs, check_vma=False
    )
```

profile of v0, /device:TPU:6, one launch (start us, length us, event | category | flops | bytes accessed | tf_op | source)
XLA Modules:
  0.0 358.6 jit_solution(18426032555463279049)
XLA Ops:
  7.2 2.3 copy.38
  9.5 8.5 %all-to-all-start = ((bf16[128,8,512]{0,2,1:T(8,128)(2,1)}), bf16[128,8,512]{0,2,1:T(8,128)(2,1)S(1)}, u32[]{:S(2)}, u32[]{:S(2)}) async-start(bf16[128,8,512]{0,2,1:T(8,128)(2,1)} %bitcast), calls=%async_computation | async-start | bytes 2097152 | tf_op jit(solution)/shard_map/all_to_all | solution.py:25
  18.0 1.3 copy.48
  19.3 27.4 %all-to-all-done = bf16[128,8,512]{0,2,1:T(8,128)(2,1)S(1)} async-done(((bf16[128,8,512]{0,2,1:T(8,128)(2,1)}), bf16[128,8,512]{0,2,1:T(8,128)(2,1)S(1)}, u32[]{:S(2)}, u32[]{:S(2)}) %all-to-all-start) | async-done | bytes 1048608 | tf_op jit(solution)/shard_map/all_to_all | solution.py:25
  46.7 3.6 all-to-all-start.5
  50.4 1.1 reduce-window.6
  52.8 26.6 %all-to-all-done.5 = bf16[128,8,512]{0,2,1:T(8,128)(2,1)S(1)} async-done(((bf16[128,8,512]{0,2,1:T(8,128)(2,1)}), bf16[128,8,512]{0,2,1:T(8,128)(2,1)S(1)}, u32[]{:S(2)}, u32[]{:S(2)}) %all-to-all-start.5) | async-done | bytes 1048608 | tf_op jit(solution)/shard_map/all_to_all | solution.py:28
  80.4 1.5 copy.49
  84.3 1.3 copy.40
  85.6 3.6 all-to-all-start.1
  89.2 2.3 copy.42
  91.5 26.9 %all-to-all-done.1 = bf16[128,8,512]{0,2,1:T(8,128)(2,1)S(1)} async-done(((bf16[128,8,512]{0,2,1:T(8,128)(2,1)}), bf16[128,8,512]{0,2,1:T(8,128)(2,1)S(1)}, u32[]{:S(2)}, u32[]{:S(2)}) %all-to-all-start.1) | async-done | bytes 1048608 | tf_op jit(solution)/shard_map/all_to_all | solution.py:26
  118.4 3.6 %all-to-all-start.2 = ((bf16[128,8,512]{0,2,1:T(8,128)(2,1)}), bf16[128,8,512]{0,2,1:T(8,128)(2,1)S(1)}, u32[]{:S(2)}, u32[]{:S(2)}) async-start(bf16[128,8,512]{0,2,1:T(8,128)(2,1)} %bitcast.7), calls=%async_computation.2 | async-start | bytes 2097152 | tf_op jit(solution)/shard_map/all_to_all | solution.py:27
  122.0 1.5 copy.41
  123.5 27.6 %all-to-all-done.2 = bf16[128,8,512]{0,2,1:T(8,128)(2,1)S(1)} async-done(((bf16[128,8,512]{0,2,1:T(8,128)(2,1)}), bf16[128,8,512]{0,2,1:T(8,128)(2,1)S(1)}, u32[]{:S(2)}, u32[]{:S(2)}) %all-to-all-start.2) | async-done | bytes 1048608 | tf_op jit(solution)/shard_map/all_to_all | solution.py:27
  152.1 1.5 copy.43
  156.6 7.8 %all-to-all-start.3 = ((f32[32,1,4]{2,1,0:T(1,128)}), f32[32,1,4]{2,1,0:T(1,128)S(1)}, u32[]{:S(2)}, u32[]{:S(2)}) async-start(f32[32,1,4]{2,1,0:T(1,128)} %broadcast_in_dim.57), calls=%async_computation.3 | async-start | bytes 32768 | tf_op jit(solution)/shard_map/all_to_all | solution.py:9
  164.5 5.2 %all-to-all-done.3 = f32[32,1,4]{2,1,0:T(1,128)S(1)} async-done(((f32[32,1,4]{2,1,0:T(1,128)}), f32[32,1,4]{2,1,0:T(1,128)S(1)}, u32[]{:S(2)}, u32[]{:S(2)}) %all-to-all-start.3) | async-done | bytes 544 | tf_op jit(solution)/shard_map/all_to_all | solution.py:9
  170.0 2.2 multiply_convert_fusion
  172.2 1.9 multiply_convert_fusion.4
  174.2 2.2 multiply_convert_fusion.1
  176.3 2.2 multiply_convert_fusion.5
  178.5 2.1 multiply_convert_fusion.2
  180.6 2.2 multiply_convert_fusion.6
  182.9 2.2 multiply_convert_fusion.3
  185.1 2.1 multiply_convert_fusion.7
  187.2 3.1 multiply_reduce_fusion
  190.3 1.0 fusion.5
  191.3 1.0 fusion.6
  192.4 1.1 fusion.7
  194.5 8.6 %all-gather.3.cloned.1.call-done = bf16[32,4,128,128]{3,2,1,0:T(8,128)(2,1)} async-done(((bf16[1,4,128,128]{3,2,1,0:T(8,128)(2,1)}), bf16[32,4,128,128]{3,2,1,0:T(8,128)(2,1)}) %all-gather.3.cloned.1.call-update) | async-done | bytes 4194320 | tf_op jit(solution)/shard_map/all_gather | solution.py:80
  203.1 3.2 multiply_reduce_fusion.1
  208.4 1.6 fusion.23
  210.5 1.5 fusion.22
  213.3 1.2 copy_bitcast_fusion.1
  214.5 7.0 %all-to-all-start.7 = ((bf16[8,128,512]{1,2,0:T(8,128)(2,1)}), bf16[8,128,512]{1,2,0:T(8,128)(2,1)}, u32[]{:S(2)}, u32[]{:S(2)}) async-start(bf16[8,128,512]{1,2,0:T(8,128)(2,1)} %copy_bitcast_fusion.1), calls=%async_computation.7 | async-start | bytes 2097152 | tf_op jit(solution)/shard_map/all_to_all | solution.py:148
  221.5 1.3 fusion.10
  222.9 2.5 fusion.21
  225.4 1.8 fusion.20
  227.2 1.2 copy_bitcast_fusion.2
  228.4 1.0 fusion.1
  229.4 1.0 fusion.2
  230.5 1.0 fusion.3
  231.5 1.0 fusion
  232.6 18.2 %all-to-all-done.7 = bf16[8,128,512]{1,2,0:T(8,128)(2,1)} async-done(((bf16[8,128,512]{1,2,0:T(8,128)(2,1)}), bf16[8,128,512]{1,2,0:T(8,128)(2,1)}, u32[]{:S(2)}, u32[]{:S(2)}) %all-to-all-start.7) | async-done | bytes 1048608 | tf_op jit(solution)/shard_map/all_to_all | solution.py:148
  250.8 4.2 %all-to-all-start.6 = ((bf16[8,128,512]{1,2,0:T(8,128)(2,1)}), bf16[8,128,512]{1,2,0:T(8,128)(2,1)}, u32[]{:S(2)}, u32[]{:S(2)}) async-start(bf16[8,128,512]{1,2,0:T(8,128)(2,1)} %copy_bitcast_fusion.2), calls=%async_computation.6 | async-start | bytes 2097152 | tf_op jit(solution)/shard_map/all_to_all | solution.py:147
  255.1 1.8 fusion.31
  257.1 1.7 fusion.30
  259.8 1.2 copy_bitcast_fusion
  261.0 1.0 fusion.12
  262.1 1.0 fusion.13
  263.1 21.1 %all-to-all-done.6 = bf16[8,128,512]{1,2,0:T(8,128)(2,1)} async-done(((bf16[8,128,512]{1,2,0:T(8,128)(2,1)}), bf16[8,128,512]{1,2,0:T(8,128)(2,1)}, u32[]{:S(2)}, u32[]{:S(2)}) %all-to-all-start.6) | async-done | bytes 1048608 | tf_op jit(solution)/shard_map/all_to_all | solution.py:147
  284.2 4.2 %all-to-all-start.8 = ((bf16[8,128,512]{1,2,0:T(8,128)(2,1)}), bf16[8,128,512]{1,2,0:T(8,128)(2,1)}, u32[]{:S(2)}, u32[]{:S(2)}) async-start(bf16[8,128,512]{1,2,0:T(8,128)(2,1)} %copy_bitcast_fusion), calls=%async_computation.8 | async-start | bytes 2097152 | tf_op jit(solution)/shard_map/all_to_all | solution.py:149
  288.5 1.3 fusion.14
  289.9 1.3 fusion.15
  291.2 2.0 fusion.19
  295.8 1.2 copy_bitcast_fusion.3
  297.0 20.8 %all-to-all-done.8 = bf16[8,128,512]{1,2,0:T(8,128)(2,1)} async-done(((bf16[8,128,512]{1,2,0:T(8,128)(2,1)}), bf16[8,128,512]{1,2,0:T(8,128)(2,1)}, u32[]{:S(2)}, u32[]{:S(2)}) %all-to-all-start.8) | async-done | bytes 1048608 | tf_op jit(solution)/shard_map/all_to_all | solution.py:149
  317.7 3.6 all-to-all-start.4
  321.3 2.3 copy.56
  323.6 2.3 copy.55
  325.8 2.3 copy.57
  328.1 22.4 %all-to-all-done.4 = bf16[8,128,512]{1,2,0:T(8,128)(2,1)S(1)} async-done(((bf16[8,128,512]{1,2,0:T(8,128)(2,1)}), bf16[8,128,512]{1,2,0:T(8,128)(2,1)S(1)}, u32[]{:S(2)}, u32[]{:S(2)}) %all-to-all-start.4) | async-done | bytes 1048608 | tf_op jit(solution)/shard_map/all_to_all | solution.py:146
  350.5 1.3 copy.54
  (129 shorter events, 17.7 us)
Async XLA Ops:
  7.2 10.8 %copy-start.34 = (bf16[128,4096]{1,0:T(8,128)(2,1)S(1)}, bf16[128,4096]{1,0:T(8,128)(2,1)}, u32[]{:S(2)}) copy-start(bf16[128,4096]{1,0:T(8,128)(2,1)} %param.8) | copy-start | bytes 3145732
  7.2 43.2 %copy-start.38 = (f32[4,1024]{1,0:T(4,128)S(1)}, f32[4,1024]{1,0:T(4,128)}, u32[]{:S(2)}) copy-start(f32[4,1024]{1,0:T(4,128)} %param.9) | copy-start | bytes 49156
  9.5 37.2 %all-to-all-start = ((bf16[128,8,512]{0,2,1:T(8,128)(2,1)}), bf16[128,8,512]{0,2,1:T(8,128)(2,1)S(1)}, u32[]{:S(2)}, u32[]{:S(2)}) async-start(bf16[128,8,512]{0,2,1:T(8,128)(2,1)} %bitcast), calls=%async_computation | async-start | bytes 2097152 | tf_op jit(solution)/shard_map/all_to_all | solution.py:25
  46.7 32.7 %all-to-all-start.5 = ((bf16[128,8,512]{0,2,1:T(8,128)(2,1)}), bf16[128,8,512]{0,2,1:T(8,128)(2,1)S(1)}, u32[]{:S(2)}, u32[]{:S(2)}) async-start(bf16[128,8,512]{0,2,1:T(8,128)(2,1)} %bitcast.39), calls=%async_computation.5 | async-start | bytes 2097152 | tf_op jit(solution)/shard_map/all_to_all | solution.py:28
  50.3 136.9 %all-gather.5.cloned.1.call-start = ((), (), s32[]{:S(2)}) async-start(), calls=%async_computation.10 | async-start | bytes 4325376 | tf_op jit(solution)/shard_map/all_gather | solution.py:83
  52.8 32.9 %copy-start.15 = (bf16[8,128,512]{2,1,0:T(8,128)(2,1)}, bf16[8,128,512]{2,1,0:T(8,128)(2,1)S(1)}, u32[]{:S(2)}) copy-start(bf16[8,128,512]{2,1,0:T(8,128)(2,1)S(1)} %copy.39) | copy-start | bytes 3145732
  52.8 31.5 %copy-start.35 = (bf16[128,4096]{1,0:T(8,128)(2,1)S(1)}, bf16[128,4096]{1,0:T(8,128)(2,1)}, u32[]{:S(2)}) copy-start(bf16[128,4096]{1,0:T(8,128)(2,1)} %param.6) | copy-start | bytes 3145732
  79.4 1.0 copy-start.23
  81.9 88.1 %copy-start.19 = (bf16[8,128,512]{2,1,0:T(8,128)(2,1)}, bf16[8,128,512]{2,1,0:T(8,128)(2,1)S(1)}, u32[]{:S(2)}) copy-start(bf16[8,128,512]{2,1,0:T(8,128)(2,1)S(1)} %copy.49) | copy-start | bytes 3145732
  85.6 32.7 %all-to-all-start.1 = ((bf16[128,8,512]{0,2,1:T(8,128)(2,1)}), bf16[128,8,512]{0,2,1:T(8,128)(2,1)S(1)}, u32[]{:S(2)}, u32[]{:S(2)}) async-start(bf16[128,8,512]{0,2,1:T(8,128)(2,1)} %bitcast.249), calls=%async_computation.1 | async-start | bytes 2097152 | tf_op jit(solution)/shard_map/all_to_all | solution.py:26
  118.4 3.7 %copy-start.24 = (bf16[128,8,512]{0,2,1:T(8,128)(2,1)}, bf16[128,8,512]{0,2,1:T(8,128)(2,1)S(1)}, u32[]{:S(2)}) copy-start(bf16[128,8,512]{0,2,1:T(8,128)(2,1)S(1)} %all-to-all-done.1) | copy-start | bytes 3145732
  118.4 32.7 %all-to-all-start.2 = ((bf16[128,8,512]{0,2,1:T(8,128)(2,1)}), bf16[128,8,512]{0,2,1:T(8,128)(2,1)S(1)}, u32[]{:S(2)}, u32[]{:S(2)}) async-start(bf16[128,8,512]{0,2,1:T(8,128)(2,1)} %bitcast.7), calls=%async_computation.2 | async-start | bytes 2097152 | tf_op jit(solution)/shard_map/all_to_all | solution.py:27
  122.0 81.1 %all-gather.3.cloned.1.call-start = ((), (), s32[]{:S(2)}) async-start(), calls=%async_computation.9 | async-start | bytes 4325376 | tf_op jit(solution)/shard_map/all_gather | solution.py:80
  123.5 46.5 %copy-start.11 = (bf16[8,128,512]{2,1,0:T(8,128)(2,1)}, bf16[8,128,512]{2,1,0:T(8,128)(2,1)S(1)}, u32[]{:S(2)}) copy-start(bf16[8,128,512]{2,1,0:T(8,128)(2,1)S(1)} %copy.41) | copy-start | bytes 3145732
  151.1 1.0 copy-start.25
  156.6 13.1 %all-to-all-start.3 = ((f32[32,1,4]{2,1,0:T(1,128)}), f32[32,1,4]{2,1,0:T(1,128)S(1)}, u32[]{:S(2)}, u32[]{:S(2)}) async-start(f32[32,1,4]{2,1,0:T(1,128)} %broadcast_in_dim.57), calls=%async_computation.3 | async-start | bytes 32768 | tf_op jit(solution)/shard_map/all_to_all | solution.py:9
  170.0 2.2 copy-start.16
  172.2 1.9 copy-start.20
  174.2 2.2 copy-start.12
  203.1 3.2 copy-start.21
  203.1 4.7 %copy-start.10 = (bf16[1024,1024]{1,0:T(8,128)(2,1)S(1)}, bf16[1024,1024]{1,0:T(8,128)(2,1)}, u32[]{:S(2)}) copy-start(bf16[1024,1024]{1,0:T(8,128)(2,1)} %multiply_convert_fusion) | copy-start | bytes 6291460
  203.1 4.8 %copy-start.17 = (bf16[8,128,512]{2,1,0:T(8,128)(2,1)S(1)}, bf16[8,128,512]{2,1,0:T(8,128)(2,1)}, u32[]{:S(2)}) copy-start(bf16[8,128,512]{2,1,0:T(8,128)(2,1)} %copy-done.15) | copy-start | bytes 3145732
  203.1 4.8 %copy-start.31 = (f32[1024,128]{0,1:T(8,128)S(1)}, f32[1024,128]{0,1:T(8,128)}, u32[]{:S(2)}) copy-start(f32[1024,128]{0,1:T(8,128)} %fusion.4) | copy-start | bytes 1572868
  206.3 2.1 copy-start.13
  207.9 2.1 copy-start.9
  207.9 2.1 copy-start.30
  210.0 2.1 copy-start.6
  210.0 2.1 copy-start.27
  210.5 2.3 copy-start.7
  210.5 2.3 copy-start.26
  214.5 36.3 %all-to-all-start.7 = ((bf16[8,128,512]{1,2,0:T(8,128)(2,1)}), bf16[8,128,512]{1,2,0:T(8,128)(2,1)}, u32[]{:S(2)}, u32[]{:S(2)}) async-start(bf16[8,128,512]{1,2,0:T(8,128)(2,1)} %copy_bitcast_fusion.1), calls=%async_computation.7 | async-start | bytes 2097152 | tf_op jit(solution)/shard_map/all_to_all | solution.py:148
  221.5 3.9 %copy-start.8 = (bf16[1024,1024]{1,0:T(8,128)(2,1)S(1)}, bf16[1024,1024]{1,0:T(8,128)(2,1)}, u32[]{:S(2)}) copy-start(bf16[1024,1024]{1,0:T(8,128)(2,1)} %multiply_convert_fusion.3) | copy-start | bytes 6291460
  221.5 3.9 %copy-start.32 = (f32[1024,128]{0,1:T(8,128)S(1)}, f32[1024,128]{0,1:T(8,128)}, u32[]{:S(2)}) copy-start(f32[1024,128]{0,1:T(8,128)} %fusion.11) | copy-start | bytes 1572868
  221.5 5.7 %copy-start.36 = (bf16[1024,128]{0,1:T(8,128)(2,1)S(1)}, bf16[1024,128]{0,1:T(8,128)(2,1)}, u32[]{:S(2)}) copy-start(bf16[1024,128]{0,1:T(8,128)(2,1)} %fusion.23) | copy-start | bytes 786436
  221.5 5.7 %copy-start.37 = (bf16[1024,128]{0,1:T(8,128)(2,1)S(1)}, bf16[1024,128]{0,1:T(8,128)(2,1)}, u32[]{:S(2)}) copy-start(bf16[1024,128]{0,1:T(8,128)(2,1)} %fusion.22) | copy-start | bytes 786436
  222.9 5.5 %copy-start.14 = (bf16[8,128,512]{2,1,0:T(8,128)(2,1)S(1)}, bf16[8,128,512]{2,1,0:T(8,128)(2,1)}, u32[]{:S(2)}) copy-start(bf16[8,128,512]{2,1,0:T(8,128)(2,1)} %copy-done.11) | copy-start | bytes 3145732
  250.8 33.5 %all-to-all-start.6 = ((bf16[8,128,512]{1,2,0:T(8,128)(2,1)}), bf16[8,128,512]{1,2,0:T(8,128)(2,1)}, u32[]{:S(2)}, u32[]{:S(2)}) async-start(bf16[8,128,512]{1,2,0:T(8,128)(2,1)} %copy_bitcast_fusion.2), calls=%async_computation.6 | async-start | bytes 2097152 | tf_op jit(solution)/shard_map/all_to_all | solution.py:147
  255.0 1.8 copy-start
  255.0 2.1 copy-start.22
  255.0 3.8 %copy-start.2 = (bf16[1024,1024]{1,0:T(8,128)(2,1)S(1)}, bf16[1024,1024]{1,0:T(8,128)(2,1)}, u32[]{:S(2)}) copy-start(bf16[1024,1024]{1,0:T(8,128)(2,1)} %multiply_convert_fusion.6) | copy-start | bytes 6291460
  255.0 3.8 %copy-start.29 = (f32[1024,128]{0,1:T(8,128)S(1)}, f32[1024,128]{0,1:T(8,128)}, u32[]{:S(2)}) copy-start(f32[1024,128]{0,1:T(8,128)} %fusion.2) | copy-start | bytes 1572868
  257.1 2.2 copy-start.4
  257.1 2.2 copy-start.28
  259.3 1.7 copy-start.18
  284.2 33.5 %all-to-all-start.8 = ((bf16[8,128,512]{1,2,0:T(8,128)(2,1)}), bf16[8,128,512]{1,2,0:T(8,128)(2,1)}, u32[]{:S(2)}, u32[]{:S(2)}) async-start(bf16[8,128,512]{1,2,0:T(8,128)(2,1)} %copy_bitcast_fusion), calls=%async_computation.8 | async-start | bytes 2097152 | tf_op jit(solution)/shard_map/all_to_all | solution.py:149
  288.5 4.7 %copy-start.1 = (bf16[1024,1024]{1,0:T(8,128)(2,1)S(1)}, bf16[1024,1024]{1,0:T(8,128)(2,1)}, u32[]{:S(2)}) copy-start(bf16[1024,1024]{1,0:T(8,128)(2,1)} %multiply_convert_fusion.5) | copy-start | bytes 6291460
  288.5 4.7 %copy-start.33 = (f32[1024,128]{0,1:T(8,128)S(1)}, f32[1024,128]{0,1:T(8,128)}, u32[]{:S(2)}) copy-start(f32[1024,128]{0,1:T(8,128)} %fusion.13) | copy-start | bytes 1572868
  288.5 5.6 %copy-start.3 = (bf16[1024,1024]{1,0:T(8,128)(2,1)S(1)}, bf16[1024,1024]{1,0:T(8,128)(2,1)}, u32[]{:S(2)}) copy-start(bf16[1024,1024]{1,0:T(8,128)(2,1)} %multiply_convert_fusion.6) | copy-start | bytes 6291460
  291.2 3.7 %copy-start.5 = (bf16[1024,1024]{1,0:T(8,128)(2,1)S(1)}, bf16[1024,1024]{1,0:T(8,128)(2,1)}, u32[]{:S(2)}) copy-start(bf16[1024,1024]{1,0:T(8,128)(2,1)} %multiply_convert_fusion.7) | copy-start | bytes 6291460
  317.7 32.7 %all-to-all-start.4 = ((bf16[8,128,512]{1,2,0:T(8,128)(2,1)}), bf16[8,128,512]{1,2,0:T(8,128)(2,1)S(1)}, u32[]{:S(2)}, u32[]{:S(2)}) async-start(bf16[8,128,512]{1,2,0:T(8,128)(2,1)} %copy_bitcast_fusion.3), calls=%async_computation.4 | async-start | bytes 2097152 | tf_op jit(solution)/shard_map/all_to_all | solution.py:146
Sparse Core Ops, SparseCore 0:
  84.4 46.9 all-gather.4
  156.1 46.9 all-gather.2
where the time goes:
time: 361 us; the launch traced here: 359 us
  waiting for transfers between devices  205 us (57%)
  matrix products  54.9 us (15%)
  starting transfers between devices  46.1 us (13%)
  local copies, waits for them, and re-layouts  23.8 us (7%)
  between operations  14.9 us (4%)
  other arithmetic  14 us (4%)
    all_to_all x1, waiting for transfers between devices, on_device(): lax.all_to_all(value_rows, 'head', split_axis=1, concat_axis=0, tiled=True)  27.6 us
    all_to_all x1, waiting for transfers between devices, on_device(): lax.all_to_all(query_rows, 'head', split_axis=1, concat_axis=0, tiled=True)  27.4 us
    all_to_all x1, waiting for transfers between devices, on_device(): lax.all_to_all(key_rows, 'head', split_axis=1, concat_axis=0, tiled=True)  26.9 us
    all_to_all x1, waiting for transfers between devices, on_device(): lax.all_to_all(out_grad, 'head', split_axis=1, concat_axis=0, tiled=True)  26.6 us
    all_to_all x1, waiting for transfers between devices, on_device(): lax.all_to_all(attended, 'head', split_axis=0, concat_axis=1, tiled=True)  22.4 us
    all_to_all x1, waiting for transfers between devices, on_device(): lax.all_to_all(query_grad, 'head', split_axis=0, concat_axis=1, tiled=True)  21.1 us
    all_to_all x1, waiting for transfers between devices, on_device(): lax.all_to_all(value_grad, 'head', split_axis=0, concat_axis=1, tiled=True)  20.8 us
    all_to_all x1, waiting for transfers between devices, on_device(): lax.all_to_all(key_grad, 'head', split_axis=0, concat_axis=1, tiled=True)  18.2 us
  transfers between devices with their start and end apart: 11, of which 10 were waited for; matrix products, arithmetic and copies ran while one was open for 20% of the time, Pallas kernels for 0%

commit v1 on v0

v1 whole, which is shorter than its diff:
```python
import functools

import jax
import jax.numpy as jnp
from jax import lax
from jax.experimental import pallas as pl
from jax.experimental.pallas import tpu as pltpu
from jax.sharding import PartitionSpec as P

E = 128
SCALE = E ** -0.5
GH = 4
HC = 2
LAG = 2
ROWS = 8
MESH = pl.DeviceIdType.MESH
F32 = jnp.float32
BF16 = jnp.bfloat16


def total_wait(ref, count, sem):
    part = ref.at[pl.ds(0, count)]
    pltpu.make_async_copy(part, part, sem).wait()


def barrier_with(peers):
    barrier = pltpu.get_barrier_semaphore()
    for peer in peers:
        pl.semaphore_signal(barrier, inc=1, device_id=peer, device_id_type=MESH)
    pl.semaphore_wait(barrier, len(peers))


def decay_kernel(nz, nrow, nx, decay_ref, dz_ref, lb_ref, lx_ref, msg, dz, bl, lb, rs, lx,
                 s_dz, r_dz, s_lb, r_lb, s_lx, r_lx):
    z = lax.axis_index("head")
    sq = lax.axis_index("seq")
    x = sq // nrow
    m = sq % nrow
    z_peers = [(z + i) % nz for i in range(1, nz)]
    m_peers = [(m + i) % nrow for i in range(1, nrow)]
    x_peers = [(x + i) % nx for i in range(1, nx)]
    barrier_with([(sq, p) for p in z_peers] + [(x * nrow + p, z) for p in m_peers]
                 + [(p * nrow + m, z) for p in x_peers])
    run = decay_ref[...]
    length = run.shape[1]
    lane = lax.broadcasted_iota(jnp.int32, run.shape, 1)
    shift = 1
    while shift < length:
        run = run + jnp.where(lane >= shift, pltpu.roll(run, shift, 1), 0.0)
        shift *= 2
    block_log = jnp.broadcast_to(run[:, length - 1:], (GH, E))
    start = jnp.zeros((GH, E), F32)
    for p in range(nz):
        part = run[:, p * E:(p + 1) * E]
        end = jnp.broadcast_to(part[:, E - 1:], (GH, E))
        msg[p, 0:GH, :] = part
        msg[p, GH:2 * GH, :] = start
        msg[p, 2 * GH:3 * GH, :] = block_log
        msg[p, 3 * GH:, :] = end
        start = end
    bl[0:GH, :] = block_log
    bl[GH:, :] = jnp.zeros((8 - GH, E), F32)
    copies = []
    for i, p in enumerate(m_peers):
        copies.append(pltpu.make_async_remote_copy(
            bl, lb.at[m], s_lb.at[i], r_lb, device_id=(x * nrow + p, z), device_id_type=MESH))
        copies[-1].start()
    for i, p in enumerate(z_peers):
        copies.append(pltpu.make_async_remote_copy(
            msg.at[p], dz.at[z], s_dz.at[i], r_dz, device_id=(sq, p), device_id_type=MESH))
        copies[-1].start()
    dz[pl.ds(z, 1)] = msg[pl.ds(z, 1)]
    lb[pl.ds(m, 1)] = bl[...][None]
    total_wait(lb, nrow - 1, r_lb)
    rs[...] = jnp.sum(lb[...], axis=0)
    for i, p in enumerate(x_peers):
        copies.append(pltpu.make_async_remote_copy(
            rs, lx.at[x], s_lx.at[i], r_lx, device_id=(p * nrow + m, z), device_id_type=MESH))
        copies[-1].start()
    lx[pl.ds(x, 1)] = rs[...][None]
    total_wait(dz, nz - 1, r_dz)
    total_wait(lx, nx - 1, r_lx)
    dz_ref[...] = dz[...]
    lb_ref[...] = lb[...]
    lx_ref[...] = lx[...]
    for copy in copies:
        copy.wait_send()


def run_decay(decay, nz, nrow, nx):
    vm = pl.BlockSpec(memory_space=pltpu.VMEM)
    dma = pltpu.SemaphoreType.DMA
    return pl.pallas_call(
        functools.partial(decay_kernel, nz, nrow, nx),
        out_shape=(jax.ShapeDtypeStruct((nz, 4 * GH, E), F32),
                   jax.ShapeDtypeStruct((nrow, 8, E), F32),
                   jax.ShapeDtypeStruct((nx, 8, E), F32)),
        in_specs=[vm],
        out_specs=(vm, vm, vm),
        scratch_shapes=[
            pltpu.VMEM((nz, 4 * GH, E), F32), pltpu.VMEM((nz, 4 * GH, E), F32),
            pltpu.VMEM((8, E), F32), pltpu.VMEM((nrow, 8, E), F32),
            pltpu.VMEM((8, E), F32), pltpu.VMEM((nx, 8, E), F32),
            dma((nz - 1,)), dma, dma((nrow - 1,)), dma, dma((nx - 1,)), dma,
        ],
        compiler_params=pltpu.CompilerParams(collective_id=1, has_side_effects=True),
        name="decay_exchange",
    )(decay)


def column_of(row):
    return jnp.transpose(jnp.broadcast_to(row, (E, E)))


def tdot(a, b):
    return lax.dot_general(a, b, (((0,), (0,)), ((), ())), preferred_element_type=F32)


def ntdot(a, b):
    return lax.dot_general(a, b, (((1,), (1,)), ((), ())), preferred_element_type=F32)


def dot(a, b):
    return jnp.dot(a, b, preferred_element_type=F32)


def update_kernel(heads, q_ref, k_ref, v_ref, g_ref, r_ref, c_ref, u_ref):
    for i in range(heads):
        cols = pl.ds(i * E, E)
        r_col = column_of(r_ref[i])
        keyed = (k_ref[:, cols].astype(F32) * jnp.exp(r_col - c_ref[i])).astype(BF16)
        queried = (q_ref[:, cols].astype(F32) * jnp.exp(-r_col)).astype(BF16)
        u_ref[0, i] = tdot(keyed, v_ref[:, cols]).astype(BF16)
        u_ref[1, i] = (SCALE * tdot(queried, g_ref[:, cols])).astype(BF16)


def run_update(q, k, v, g, r, c, heads=4):
    n = r.shape[0]
    tok = pl.BlockSpec((E, heads * E), lambda i: (0, i))
    row = pl.BlockSpec((heads, 1, E), lambda i: (i, 0, 0))
    return pl.pallas_call(
        functools.partial(update_kernel, heads),
        grid=(n // heads,),
        out_shape=jax.ShapeDtypeStruct((2, n, E, E), BF16),
        in_specs=[tok, tok, tok, tok, row, row],
        out_specs=pl.BlockSpec((2, heads, E, E), lambda i: (0, i, 0, 0)),
        name="chunk_updates",
    )(q, k, v, g, r[:, None], c[:, None])


def output_kernel(heads, q_ref, k_ref, v_ref, g_ref, r_ref, c_ref, s_ref,
                  a_ref, dq_ref, dk_ref, dv_ref):
    t_at = lax.broadcasted_iota(jnp.int32, (E, E), 0)
    s_at = lax.broadcasted_iota(jnp.int32, (E, E), 1)
    causal = t_at >= s_at
    for i in range(heads):
        cols = pl.ds(i * E, E)
        q, k, v, g = q_ref[:, cols], k_ref[:, cols], v_ref[:, cols], g_ref[:, cols]
        r_row = r_ref[i]
        r_col = column_of(r_row)
        mask = jnp.where(causal, jnp.exp(jnp.where(causal, r_row - r_col, 0.0)), 0.0) * SCALE
        growth = SCALE * jnp.exp(-r_col)
        weight = jnp.exp(r_col - c_ref[i])
        scores = (ntdot(q, k) * mask).astype(BF16)
        grads = (ntdot(g, v) * mask).astype(BF16)
        state, back = s_ref[0, i], s_ref[1, i]
        a_ref[:, cols] = (dot(scores, v) + growth * dot(q, state)).astype(BF16)
        dq_ref[:, cols] = (dot(grads, k) + growth * ntdot(g, state)).astype(BF16)
        dk_ref[:, cols] = (tdot(grads, q) + weight * ntdot(v, back)).astype(BF16)
        dv_ref[:, cols] = (tdot(scores, g) + weight * dot(k, back)).astype(BF16)


def run_output(q, k, v, g, r, c, states, heads=4):
    n = r.shape[0]
    tok = pl.BlockSpec((E, heads * E), lambda i: (0, i))
    row = pl.BlockSpec((heads, 1, E), lambda i: (i, 0, 0))
    return pl.pallas_call(
        functools.partial(output_kernel, heads),
        grid=(n // heads,),
        out_shape=(jax.ShapeDtypeStruct(q.shape, BF16),) * 4,
        in_specs=[tok, tok, tok, tok, row, row,
                  pl.BlockSpec((2, heads, E, E), lambda i: (0, i, 0, 0))],
        out_specs=(tok, tok, tok, tok),
        name="chunk_outputs",
    )(q, k, v, g, r[:, None], c[:, None], states)


def state_kernel(nz, nrow, nx, plan, u_ref, chain_ref, suf_ref, pre_ref, eb_ref, ex_ref, out_ref,
                 rs_in, rs_out, tot, ta, rxo, rx, so, sa, ch_in, ch_out,
                 rs_s, rs_r, ta_s, ta_r, rx_s, rx_r, so_s, so_r, ag_s, ag_r, ch_s, ch_r):
    z = lax.axis_index("head")
    sq = lax.axis_index("seq")
    x = sq // nrow
    m = sq % nrow
    right = (z + 1) % nz
    left = (z + nz - 1) % nz
    heads = nz * GH
    chunks = heads // HC
    cut = E // nrow
    toward = ((sq, right), (sq, left))
    m_peers = [(m + i) % nrow for i in range(1, nrow)]
    x_peers = [(x + i) % nx for i in range(1, nx)]
    barrier_with(list(toward) + [(x * nrow + p, z) for p in m_peers] + [(p * nrow + m, z) for p in x_peers])

    before = (suf_ref, pre_ref)
    after = (pre_ref, suf_ref)
    pending = []

    def hops(way, t):
        return nz // 2 if way == t else nz // 2 - 1

    def sign(way):
        return 1 if way == 0 else -1

    for t in range(2):
        place = z if t == 0 else nz - 1 - z

        @pl.when(place == 0)
        def _(t=t):
            def clear(h, _):
                ch_in[t, h] = jnp.zeros((E, E), BF16)
                return 0
            lax.fori_loop(0, heads, clear, 0)

    def chain_copy(t, c):
        part = pl.ds(c * HC, HC)
        return pltpu.make_async_remote_copy(
            ch_out.at[t, part], ch_in.at[t, part], ch_s.at[t, c], ch_r.at[t, c],
            device_id=toward[t], device_id_type=MESH)

    def chain_step(step, _):
        for t in range(2):
            place = z if t == 0 else nz - 1 - z
            c = step - LAG * place

            @pl.when((c >= 0) & (c < chunks))
            def _(t=t, place=place, c=c):
                @pl.when(place > 0)
                def _():
                    chain_copy(t, c).wait_recv()

                @pl.when(place < nz - 1)
                def _():
                    for i in range(HC):
                        h = c * HC + i
                        nxt = chain_ref[h] * ch_in[t, h].astype(F32) + u_ref[t, h].astype(F32)
                        ch_out[t, h] = nxt.astype(BF16)
                    chain_copy(t, c).start()
        return 0

    chain_at = [0]

    def chain_run(count):
        if count > 0:
            lax.fori_loop(chain_at[0], chain_at[0] + count, chain_step, 0)
            chain_at[0] += count

    for s in range(nz // 2):
        for t in range(2):
            for way in range(2):
                k = hops(way, t)
                if s >= k:
                    continue
                group = (z + sign(way) * (k - s) + nz) % nz
                if s > 0:
                    pltpu.make_async_remote_copy(
                        rs_out.at[way, t, s - 1], rs_in.at[way, t, s - 1], rs_s.at[way, t, s - 1],
                        rs_r.at[way, t, s - 1], device_id=toward[way], device_id_type=MESH).wait_recv()

                def fill(i, _, way=way, t=t, s=s, group=group):
                    h = group * GH + i
                    val = before[t][h] * u_ref[t, h].astype(F32)
                    if s > 0:
                        val = val + rs_in[way, t, s - 1, i].astype(F32)
                    rs_out[way, t, s, i] = val.astype(BF16)
                    return 0
                lax.fori_loop(0, GH, fill, 0)
                copy = pltpu.make_async_remote_copy(
                    rs_out.at[way, t, s], rs_in.at[way, t, s], rs_s.at[way, t, s], rs_r.at[way, t, s],
                    device_id=toward[way], device_id_type=MESH)
                copy.start()
                pending.append(copy)
        chain_run(plan[0][s])
    for t in range(2):
        for way in range(2):
            k = hops(way, t)
            pltpu.make_async_remote_copy(
                rs_out.at[way, t, k - 1], rs_in.at[way, t, k - 1], rs_s.at[way, t, k - 1],
                rs_r.at[way, t, k - 1], device_id=toward[way], device_id_type=MESH).wait_recv()

        def finish(i, _, t=t):
            h = z * GH + i
            val = before[t][h] * u_ref[t, h].astype(F32)
            for way in range(2):
                val = val + rs_in[way, t, hops(way, t) - 1, i].astype(F32)
            tot[t, i] = val.astype(BF16)
            return 0
        lax.fori_loop(0, GH, finish, 0)

    for i, p in enumerate(m_peers):
        copy = pltpu.make_async_remote_copy(
            tot.at[:, :, pl.ds(p * cut, cut), :], ta.at[m], ta_s.at[i], ta_r,
            device_id=(x * nrow + p, z), device_id_type=MESH)
        copy.start()
        pending.append(copy)
    ta[pl.ds(m, 1)] = tot[:, :, pl.ds(pl.multiple_of(m * cut, cut), cut), :][None]
    chain_run(plan[1][0])
    total_wait(ta, nrow - 1, ta_r)
    order = (list(range(nrow)), list(range(nrow))[::-1])
    for t in range(2):
        for i in range(GH):
            acc = ta[order[t][0], t, i].astype(F32)
            for b in order[t][1:]:
                acc = eb_ref[b, i:i + 1, :] * acc + ta[b, t, i].astype(F32)
            rxo[t, i] = acc.astype(BF16)
    for i, p in enumerate(x_peers):
        copy = pltpu.make_async_remote_copy(
            rxo, rx.at[x], rx_s.at[i], rx_r, device_id=(p * nrow + m, z), device_id_type=MESH)
        copy.start()
        pending.append(copy)
    chain_run(plan[1][1])
    total_wait(rx, nx - 1, rx_r)
    for t in range(2):
        for i in range(GH):
            acc = jnp.zeros((cut, E), F32)
            for b in (range(nx) if t == 0 else range(nx - 1, -1, -1)):
                use = (b < x) if t == 0 else (b > x)
                new = ex_ref[b, i:i + 1, :] * acc + rx[b, t, i].astype(F32)
                acc = jnp.where(use, new, acc)
            for b in order[t]:
                so[b, t, i] = acc.astype(BF16)
                acc = eb_ref[b, i:i + 1, :] * acc + ta[b, t, i].astype(F32)
    rows = pl.ds(pl.multiple_of(m * cut, cut), cut)
    for i, p in enumerate(m_peers):
        copy = pltpu.make_async_remote_copy(
            so.at[p], sa.at[z, :, :, rows, :], so_s.at[i], so_r,
            device_id=(x * nrow + p, z), device_id_type=MESH)
        copy.start()
        pending.append(copy)
    sa[pl.ds(z, 1), :, :, rows, :] = so[pl.ds(m, 1)]
    chain_run(plan[1][2])
    total_wait(so, nrow - 1, so_r)

    for s in range(nz // 2):
        for t in range(2):
            for way in range(2):
                k = hops(way, t)
                if s >= k:
                    continue
                group = (z - sign(way) * s + nz) % nz

                def ag_copy(group, at, way=way, t=t):
                    return pltpu.make_async_remote_copy(
                        sa.at[group, t], sa.at[group, t], ag_s.at[way, t, at], ag_r.at[way, t, at],
                        device_id=toward[way], device_id_type=MESH)
                if s > 0:
                    ag_copy(group, s - 1).wait_recv()
                copy = ag_copy(group, s)
                copy.start()
                pending.append(copy)
        chain_run(plan[2][s])
    chain_run(chunks + LAG * (nz - 1) - chain_at[0])
    for t in range(2):
        for way in range(2):
            k = hops(way, t)
            group = (z - sign(way) * k + nz) % nz
            pltpu.make_async_remote_copy(
                sa.at[group, t], sa.at[group, t], ag_s.at[way, t, k - 1], ag_r.at[way, t, k - 1],
                device_id=toward[way], device_id_type=MESH).wait_recv()

        def combine(h, _, t=t):
            val = after[t][h] * sa[h // GH, t, h % GH].astype(F32) + ch_in[t, h].astype(F32)
            out_ref[t, h] = val.astype(BF16)
            return 0
        lax.fori_loop(0, heads, combine, 0)

    for copy in pending:
        copy.wait_send()

    def drain(c, _):
        for t in range(2):
            place = z if t == 0 else nz - 1 - z

            @pl.when(place < nz - 1)
            def _(t=t):
                chain_copy(t, c).wait_send()
        return 0
    lax.fori_loop(0, chunks, drain, 0)


PLAN = ((1, 2, 3, 4), (4, 4, 4), (4, 4, 2, 0))


def run_state(u, chain, suf, pre, eb, ex, nz, nrow, nx, plan=PLAN):
    heads = nz * GH
    chunks = heads // HC
    cut = E // nrow
    half = nz // 2
    vm = pl.BlockSpec(memory_space=pltpu.VMEM)
    dma = pltpu.SemaphoreType.DMA
    return pl.pallas_call(
        functools.partial(state_kernel, nz, nrow, nx, plan),
        out_shape=jax.ShapeDtypeStruct((2, heads, E, E), BF16),
        in_specs=[vm] * 6,
        out_specs=vm,
        scratch_shapes=[
            pltpu.VMEM((2, 2, half, GH, E, E), BF16),
            pltpu.VMEM((2, 2, half, GH, E, E), BF16),
            pltpu.VMEM((2, GH, E, E), BF16),
            pltpu.VMEM((nrow, 2, GH, cut, E), BF16),
            pltpu.VMEM((2, GH, cut, E), BF16),
            pltpu.VMEM((nx, 2, GH, cut, E), BF16),
            pltpu.VMEM((nrow, 2, GH, cut, E), BF16),
            pltpu.VMEM((nz, 2, GH, E, E), BF16),
            pltpu.VMEM((2, heads, E, E), BF16),
            pltpu.VMEM((2, heads, E, E), BF16),
            dma((2, 2, half)), dma((2, 2, half)),
            dma((nrow - 1,)), dma,
            dma((nx - 1,)), dma,
            dma((nrow - 1,)), dma,
            dma((2, 2, half)), dma((2, 2, half)),
            dma((2, chunks)), dma((2, chunks)),
        ],
        compiler_params=pltpu.CompilerParams(collective_id=2, has_side_effects=True),
        name="state_scan",
    )(u, chain[:, None], suf[:, None], pre[:, None], eb, ex)


def on_device(nz, nrow, nx, q, k, v, g, decay):
    heads = nz * GH
    dz, lb, lx = run_decay(decay, nz, nrow, nx)
    run, start, block, end = (dz[:, i * GH:(i + 1) * GH].reshape(heads, E) for i in range(4))
    r = run - start
    c = end - start
    chain = jnp.exp(-c)
    suf = jnp.exp(end - block)
    pre = jnp.exp(-start)
    u = run_update(q, k, v, g, r, c)
    states = run_state(u, chain, suf, pre, jnp.exp(-lb), jnp.exp(-lx), nz, nrow, nx)
    return run_output(q, k, v, g, r, c, states)


def solution(mesh):
    nz = mesh.shape["head"]
    nrow = ROWS
    nx = mesh.shape["seq"] // nrow
    tok = P(("seq", "head"), None)
    return jax.shard_map(
        functools.partial(on_device, nz, nrow, nx), mesh=mesh,
        in_specs=(tok, tok, tok, tok, P("head", "seq")),
        out_specs=(tok,) * 4, check_vma=False)
```

time: 361 us -> 139 us (0.39)
  waiting for transfers between devices: 205 us -> 0 us
  Pallas kernels: 0 us -> 131 us
  matrix products: 54.9 us -> 0 us
  starting transfers between devices: 46.1 us -> 0 us
  local copies, waits for them, and re-layouts: 23.8 us -> 0.01 us
  between operations: 14.9 us -> 0.65 us
  other arithmetic: 14 us -> 4.79 us
    all_to_all x9 -> x0, waiting for transfers between devices: 196 us -> none  [the longest x1 27.6 us: on_device(): lax.all_to_all(value_rows, 'head', split_axis=1, concat_axis=0, tiled=True)]
    pallas_call x0 -> x4, Pallas kernels: none -> 131 us  [the longest x1 94.6 us: run_state(): pl.pallas_call(functools.partial(state_kernel, nz, nrow, nx, plan), out_s...]
    dot_general x48 -> x0, matrix products: 54.9 us -> none  [the longest x4 8.69 us: on_device(): jnp.dot(grad_head, value_head.T, preferred_element_type=jnp.float32)]
    all_to_all x9 -> x0, starting transfers between devices: 46 us -> none  [the longest x1 8.47 us: on_device(): lax.all_to_all(query_rows, 'head', split_axis=1, concat_axis=0, tiled=True)]
    unnamed x89 -> x2, local copies, waits for them, and re-layouts: 17.8 us -> 0.01 us
    all_gather x2 -> x0, waiting for transfers between devices: 8.64 us -> none  [the longest x1 8.64 us: on_device(): lax.all_gather(update_stack[None].astype(jnp.bfloat16), 'seq', axis=0, ti...]
    reduce_sum x2 -> x0, other arithmetic: 6.26 us -> none  [the longest x1 3.21 us: on_device(): jnp.sum(forward_weight[:, :, None, None] * update_piece, axis=0)]
    all_to_all x5 -> x0, local copies, waits for them, and re-layouts: 5.06 us -> none  [the longest x1 1.49 us: on_device(): lax.all_to_all(key_rows, 'head', split_axis=1, concat_axis=0, tiled=True)]
  transfers between devices with their start and end apart: 11 -> 0, of which waited for: 10 -> 0; matrix products, arithmetic and copies ran while one was open for 20% -> 0% of each run, Pallas kernels for 0% -> 0%
where the time goes in v1:
time: 139 us; the launch traced here: 137 us
  Pallas kernels  131 us (94%)
  other arithmetic  4.79 us (3%)
    pallas_call x1, Pallas kernels, run_state(): pl.pallas_call(functools.partial(state_kernel, nz, nrow, nx, plan), out_s...  94.6 us
    pallas_call x1, Pallas kernels, run_decay(): pl.pallas_call(functools.partial(decay_kernel, nz, nrow, nx), out_shape=(...  17.4 us
    pallas_call x1, Pallas kernels, run_output(): pl.pallas_call(functools.partial(output_kernel, heads), grid=(n // heads,...  11.7 us
    pallas_call x1, Pallas kernels, run_update(): pl.pallas_call(functools.partial(update_kernel, heads), grid=(n // heads,...  7.5 us

profile of v1, /device:TPU:6, one launch (start us, length us, event | category | flops | bytes accessed | tf_op | source)
XLA Modules:
  0.0 136.7 jit_solution(17029833990659766238)
XLA Ops:
  0.6 17.4 %decay_exchange.1 = (f32[8,16,128]{2,1,0:T(8,128)}, f32[8,8,128]{2,1,0:T(8,128)}, f32[4,8,128]{2,1,0:T(8,128)}) custom-call(f32[4,1024]{1,0:T(4,128)} %decay_ref.1), custom_call_target="tpu_custom_call" | custom-call | tf_op jit(solution)/shard_map/decay_exchange/pallas_call | solution.py:93
  18.1 1.5 %negate_exponential_fusion.2 = (f32[8,4,128]{2,1,0:T(4,128)}, f32[8,4,128]{2,1,0:T(4,128)}, f32[8,4,128]{2,1,0:T(4,128)S(1)}, f32[8,4,128]{2,1,0:T(4,128)}) fusion(f32[8,16,128]{2,1,0:T(8,128)} %get-tuple-element.7), kind=kLoop, calls=%fused_computation.2 | loop fusion | flops 16384 | bytes 131072 | tf_op jit(solution)/shard_map/exp | solution.py:437
  19.6 0.0 copy-start
  19.6 0.6 negate_exponential_fusion.3
  20.2 1.3 negate_exponential_fusion.1.ex_ref
  21.5 1.4 %negate_exponential_fusion.eb_ref = f32[8,8,128]{2,1,0:T(8,128)} fusion(f32[8,8,128]{2,1,0:T(8,128)} %get-tuple-element.8), kind=kLoop, calls=%fused_computation | loop fusion | flops 8192 | bytes 65536 | tf_op jit(solution)/shard_map/exp | solution.py:439
  22.9 0.0 copy-done
  22.9 7.5 %chunk_updates.1.u_ref = bf16[2,32,128,128]{3,2,1,0:T(8,128)(2,1)} custom-call(bf16[128,4096]{1,0:T(8,128)(2,1)} %q_ref.3, bf16[128,4096]{1,0:T(8,128)(2,1)} %k_ref.3, bf16[128,4096]{1,0:T(8,128)(2,1)} %v_ref.3, bf16[128,4096]{1,0:T(8,128)(2,1)} %g_ref.3, f32[32,1,128]{2,1,0:T(1,128)} %bitcast.9, f32[32,1,128]{2,1,0:T(1,128)} %bitcast.7), custom_call_target="tpu_custom_call" | custom-call | tf_op jit(solution)/shard_map/chunk_updates/pallas_call | solution.py:141
  30.4 94.6 %state_scan.1.s_ref = bf16[2,32,128,128]{3,2,1,0:T(8,128)(2,1)} custom-call(bf16[2,32,128,128]{3,2,1,0:T(8,128)(2,1)} %chunk_updates.1.u_ref, f32[32,1,128]{2,1,0:T(1,128)} %bitcast.11, f32[32,1,128]{2,1,0:T(1,128)} %bitcast.13, f32[32,1,128]{2,1,0:T(1,128)} %bitcast.12, f32[8,8,128]{2,1,0:T(8,128)} %negate_exponential_fusion.eb_ref, ...), custom_call_target="tpu_custom_call" | custom-call | tf_op jit(solution)/shard_map/state_scan/pallas_call | solution.py:401
  125.0 11.7 %chunk_outputs.1 = (bf16[128,4096]{1,0:T(8,128)(2,1)}, bf16[128,4096]{1,0:T(8,128)(2,1)}, bf16[128,4096]{1,0:T(8,128)(2,1)}, bf16[128,4096]{1,0:T(8,128)(2,1)}) custom-call(bf16[128,4096]{1,0:T(8,128)(2,1)} %q_ref.3, bf16[128,4096]{1,0:T(8,128)(2,1)} %k_ref.3, bf16[128,4096]{1,0:T(8,128)(2,1)} %v_ref.3, bf16[128,4096]{1,0:T(8,128)(2,1)} %g_ref.3, ...), custom_call_target="tpu_custom_call" | custom-call | tf_op jit(solution)/shard_map/chunk_outputs/pallas_call | solution.py:177
Async XLA Ops:
  19.6 3.3 %copy-start = (f32[8,4,128]{2,1,0:T(4,128)}, f32[8,4,128]{2,1,0:T(4,128)S(1)}, u32[]{:S(2)}) copy-start(f32[8,4,128]{2,1,0:T(4,128)S(1)} %get-tuple-element.12) | copy-start | bytes 49156

commit v2 on v1

v2 whole, which is shorter than its diff:
```python
import functools

import jax
import jax.numpy as jnp
from jax import lax
from jax.experimental import pallas as pl
from jax.experimental.pallas import tpu as pltpu
from jax.sharding import PartitionSpec as P

E = 128
SCALE = E ** -0.5
GH = 4
HC = 2
LAG = 2
ROWS = 8
MESH = pl.DeviceIdType.MESH
F32 = jnp.float32
BF16 = jnp.bfloat16


def total_wait(ref, count, sem):
    part = ref.at[pl.ds(0, count)]
    pltpu.make_async_copy(part, part, sem).wait()


def barrier_with(peers):
    barrier = pltpu.get_barrier_semaphore()
    for peer in peers:
        pl.semaphore_signal(barrier, inc=1, device_id=peer, device_id_type=MESH)
    pl.semaphore_wait(barrier, len(peers))


def column_of(row):
    return jnp.transpose(jnp.broadcast_to(row, (E, E)))


def tdot(a, b):
    return lax.dot_general(a, b, (((0,), (0,)), ((), ())), preferred_element_type=F32)


def ntdot(a, b):
    return lax.dot_general(a, b, (((1,), (1,)), ((), ())), preferred_element_type=F32)


def dot(a, b):
    return jnp.dot(a, b, preferred_element_type=F32)


def state_kernel(nz, nrow, nx, plan, q_ref, k_ref, v_ref, g_ref, decay_ref,
                 out_ref, sc_ref, rc_ref,
                 msg, dz, bl, lb, rs, lx, eb, ex, fac, u,
                 rs_in, rs_out, tot, ta, rxo, rx, so, sa, ch_in, ch_out,
                 dz_s, dz_r, lb_s, lb_r, lx_s, lx_r,
                 rs_s, rs_r, ta_s, ta_r, rx_s, rx_r, so_s, so_r, ag_s, ag_r, ch_s, ch_r):
    z = lax.axis_index("head")
    sq = lax.axis_index("seq")
    x = sq // nrow
    m = sq % nrow
    right = (z + 1) % nz
    left = (z + nz - 1) % nz
    heads = nz * GH
    chunks = heads // HC
    cut = E // nrow
    toward = ((sq, right), (sq, left))
    z_peers = [(z + i) % nz for i in range(1, nz)]
    m_peers = [(m + i) % nrow for i in range(1, nrow)]
    x_peers = [(x + i) % nx for i in range(1, nx)]
    barrier_with([(sq, p) for p in z_peers] + [(x * nrow + p, z) for p in m_peers]
                 + [(p * nrow + m, z) for p in x_peers])
    pending = []

    run = decay_ref[...]
    length = run.shape[1]
    lane = lax.broadcasted_iota(jnp.int32, run.shape, 1)
    shift = 1
    while shift < length:
        run = run + jnp.where(lane >= shift, pltpu.roll(run, shift, 1), 0.0)
        shift *= 2
    block_log = jnp.broadcast_to(run[:, length - 1:], (GH, E))
    start = jnp.zeros((GH, E), F32)
    for p in range(nz):
        part = run[:, p * E:(p + 1) * E]
        end = jnp.broadcast_to(part[:, E - 1:], (GH, E))
        msg[p, 0:GH, :] = part - start
        msg[p, GH:2 * GH, :] = start
        msg[p, 2 * GH:3 * GH, :] = block_log - end
        msg[p, 3 * GH:, :] = end - start
        start = end
    bl[0:GH, :] = block_log
    bl[GH:, :] = jnp.zeros((8 - GH, E), F32)
    for i, p in enumerate(z_peers):
        pending.append(pltpu.make_async_remote_copy(
            msg.at[p], dz.at[z], dz_s.at[i], dz_r, device_id=(sq, p), device_id_type=MESH))
        pending[-1].start()
    for i, p in enumerate(m_peers):
        pending.append(pltpu.make_async_remote_copy(
            bl, lb.at[m], lb_s.at[i], lb_r, device_id=(x * nrow + p, z), device_id_type=MESH))
        pending[-1].start()
    dz[pl.ds(z, 1)] = msg[pl.ds(z, 1)]
    lb[pl.ds(m, 1)] = bl[...][None]

    def hops(way, t):
        return nz // 2 if way == t else nz // 2 - 1

    def sign(way):
        return 1 if way == 0 else -1

    for t in range(2):
        place = z if t == 0 else nz - 1 - z

        @pl.when(place == 0)
        def _(t=t):
            def clear(h, _):
                ch_in[t, h] = jnp.zeros((E, E), BF16)
                return 0
            lax.fori_loop(0, heads, clear, 0)

    total_wait(dz, nz - 1, dz_r)
    for p in range(nz):
        for i in range(GH):
            rc_ref[p * GH + i, 0:1, :] = dz[p, i:i + 1, :]
            rc_ref[p * GH + i, 1:2, :] = dz[p, 3 * GH + i:3 * GH + i + 1, :]
            fac[p * GH + i, 0:1, :] = jnp.exp(-dz[p, GH + i:GH + i + 1, :])
            fac[p * GH + i, 1:2, :] = jnp.exp(-dz[p, 2 * GH + i:2 * GH + i + 1, :])
            fac[p * GH + i, 2:3, :] = jnp.exp(-dz[p, 3 * GH + i:3 * GH + i + 1, :])

    def before(t, h):
        return fac[h, 1 - t:2 - t, :]

    def after(t, h):
        return fac[h, t:t + 1, :]

    done = set()

    def update_group(off):
        off %= nz
        if off in done:
            return
        done.add(off)
        group = (z + off) % nz

        def one(i, _):
            h = group * GH + i
            cols = pl.ds(pl.multiple_of(h * E, E), E)
            r_col = column_of(rc_ref[h, 0:1, :])
            keyed = (k_ref[:, cols].astype(F32) * jnp.exp(r_col - rc_ref[h, 1:2, :])).astype(BF16)
            queried = (q_ref[:, cols].astype(F32) * jnp.exp(-r_col)).astype(BF16)
            u[0, h] = tdot(keyed, v_ref[:, cols]).astype(BF16)
            u[1, h] = (SCALE * tdot(queried, g_ref[:, cols])).astype(BF16)
            return 0
        lax.fori_loop(0, GH, one, 0, unroll=True)

    filled = [0]

    def fill_run(count):
        count = min(count, heads - filled[0])
        if count <= 0:
            return
        causal = (lax.broadcasted_iota(jnp.int32, (E, E), 0) >= lax.broadcasted_iota(jnp.int32, (E, E), 1))

        def one(h, _):
            cols = pl.ds(pl.multiple_of(h * E, E), E)
            r_row = rc_ref[h, 0:1, :]
            r_col = column_of(r_row)
            mask = jnp.where(causal, jnp.exp(jnp.where(causal, r_row - r_col, 0.0)), 0.0) * SCALE
            sc_ref[0, h] = (ntdot(q_ref[:, cols], k_ref[:, cols]) * mask).astype(BF16)
            sc_ref[1, h] = (ntdot(g_ref[:, cols], v_ref[:, cols]) * mask).astype(BF16)
            return 0
        lax.fori_loop(filled[0], filled[0] + count, one, 0)
        filled[0] += count

    def chain_copy(t, c):
        part = pl.ds(c * HC, HC)
        return pltpu.make_async_remote_copy(
            ch_out.at[t, part], ch_in.at[t, part], ch_s.at[t, c], ch_r.at[t, c],
            device_id=toward[t], device_id_type=MESH)

    def chain_step(step, _):
        for t in range(2):
            place = z if t == 0 else nz - 1 - z
            c = step - LAG * place

            @pl.when((c >= 0) & (c < chunks))
            def _(t=t, place=place, c=c):
                @pl.when(place > 0)
                def _():
                    chain_copy(t, c).wait_recv()

                @pl.when(place < nz - 1)
                def _():
                    for i in range(HC):
                        h = c * HC + i
                        nxt = fac[h, 2:3, :] * ch_in[t, h].astype(F32) + u[t, h].astype(F32)
                        ch_out[t, h] = nxt.astype(BF16)
                    chain_copy(t, c).start()
        return 0

    chain_at = [0]
    chain_all = chunks + LAG * (nz - 1)

    def chain_run(count):
        count = min(count, chain_all - chain_at[0])
        if count > 0:
            lax.fori_loop(chain_at[0], chain_at[0] + count, chain_step, 0)
            chain_at[0] += count

    def spare(point):
        chain_run(plan[point][0])
        fill_run(plan[point][1])

    def rs_copy(way, t, s):
        return pltpu.make_async_remote_copy(
            rs_out.at[way, t, s], rs_in.at[way, t, s], rs_s.at[way, t, s], rs_r.at[way, t, s],
            device_id=toward[way], device_id_type=MESH)

    for s in range(nz // 2):
        for way, t in ((0, 0), (1, 1), (0, 1), (1, 0)):
            k = hops(way, t)
            if s >= k:
                continue
            off = sign(way) * (k - s)
            update_group(off)
            group = (z + off + nz) % nz
            if s > 0:
                rs_copy(way, t, s - 1).wait_recv()

            def fold(i, _, way=way, t=t, s=s, group=group):
                h = group * GH + i
                val = before(t, h) * u[t, h].astype(F32)
                if s > 0:
                    val = val + rs_in[way, t, s - 1, i].astype(F32)
                rs_out[way, t, s, i] = val.astype(BF16)
                return 0
            lax.fori_loop(0, GH, fold, 0)
            pending.append(rs_copy(way, t, s))
            pending[-1].start()
            if s > 0:
                chain_run(plan[s][0])
        if s == 0:
            for off in range(nz // 2, -1, -1):
                update_group(off)
                update_group(-off)
            total_wait(lb, nrow - 1, lb_r)
            rs[...] = jnp.sum(lb[...], axis=0)
            eb[...] = jnp.exp(-lb[...])
            for i, p in enumerate(x_peers):
                pending.append(pltpu.make_async_remote_copy(
                    rs, lx.at[x], lx_s.at[i], lx_r, device_id=(p * nrow + m, z), device_id_type=MESH))
                pending[-1].start()
            lx[pl.ds(x, 1)] = rs[...][None]
        fill_run(plan[s][1])
    for t in range(2):
        for way in range(2):
            rs_copy(way, t, hops(way, t) - 1).wait_recv()

        def finish(i, _, t=t):
            h = z * GH + i
            val = before(t, h) * u[t, h].astype(F32)
            for way in range(2):
                val = val + rs_in[way, t, hops(way, t) - 1, i].astype(F32)
            tot[t, i] = val.astype(BF16)
            return 0
        lax.fori_loop(0, GH, finish, 0)

    for i, p in enumerate(m_peers):
        copy = pltpu.make_async_remote_copy(
            tot.at[:, :, pl.ds(p * cut, cut), :], ta.at[m], ta_s.at[i], ta_r,
            device_id=(x * nrow + p, z), device_id_type=MESH)
        copy.start()
        pending.append(copy)
    ta[pl.ds(m, 1)] = tot[:, :, pl.ds(pl.multiple_of(m * cut, cut), cut), :][None]
    total_wait(lx, nx - 1, lx_r)
    ex[...] = jnp.exp(-lx[...])
    spare(nz // 2)
    total_wait(ta, nrow - 1, ta_r)
    order = (list(range(nrow)), list(range(nrow))[::-1])
    for t in range(2):
        for i in range(GH):
            acc = ta[order[t][0], t, i].astype(F32)
            for b in order[t][1:]:
                acc = eb[b, i:i + 1, :] * acc + ta[b, t, i].astype(F32)
            rxo[t, i] = acc.astype(BF16)
    for i, p in enumerate(x_peers):
        copy = pltpu.make_async_remote_copy(
            rxo, rx.at[x], rx_s.at[i], rx_r, device_id=(p * nrow + m, z), device_id_type=MESH)
        copy.start()
        pending.append(copy)
    rx[pl.ds(x, 1)] = rxo[...][None]
    spare(nz // 2 + 1)
    total_wait(rx, nx - 1, rx_r)
    for t in range(2):
        for i in range(GH):
            acc = jnp.zeros((cut, E), F32)
            for b in (range(nx) if t == 0 else range(nx - 1, -1, -1)):
                use = (b < x) if t == 0 else (b > x)
                new = ex[b, i:i + 1, :] * acc + rx[b, t, i].astype(F32)
                acc = jnp.where(use, new, acc)
            for b in order[t]:
                so[b, t, i] = acc.astype(BF16)
                acc = eb[b, i:i + 1, :] * acc + ta[b, t, i].astype(F32)
    rows = pl.ds(pl.multiple_of(m * cut, cut), cut)
    for i, p in enumerate(m_peers):
        copy = pltpu.make_async_remote_copy(
            so.at[p], sa.at[z, :, :, rows, :], so_s.at[i], so_r,
            device_id=(x * nrow + p, z), device_id_type=MESH)
        copy.start()
        pending.append(copy)
    sa[pl.ds(z, 1), :, :, rows, :] = so[pl.ds(m, 1)]
    spare(nz // 2 + 2)
    total_wait(so, nrow - 1, so_r)

    def ag_copy(way, t, s):
        group = (z - sign(way) * s + nz) % nz
        return pltpu.make_async_remote_copy(
            sa.at[group, t], sa.at[group, t], ag_s.at[way, t, s], ag_r.at[way, t, s],
            device_id=toward[way], device_id_type=MESH)

    def ag_wait(way, t, s):
        group = (z - sign(way) * (s + 1) + 2 * nz) % nz
        pltpu.make_async_remote_copy(
            sa.at[group, t], sa.at[group, t], ag_s.at[way, t, s], ag_r.at[way, t, s],
            device_id=toward[way], device_id_type=MESH).wait_recv()

    for s in range(nz // 2):
        for t in range(2):
            for way in range(2):
                if s >= hops(way, t):
                    continue
                if s > 0:
                    ag_wait(way, t, s - 1)
                pending.append(ag_copy(way, t, s))
                pending[-1].start()
                chain_run(plan[nz // 2 + 3 + s][0])
        fill_run(plan[nz // 2 + 3 + s][1])
    chain_run(chain_all)
    fill_run(heads)
    for t in range(2):
        for way in range(2):
            ag_wait(way, t, hops(way, t) - 1)

        def combine(h, _, t=t):
            val = after(t, h) * sa[h // GH, t, h % GH].astype(F32) + ch_in[t, h].astype(F32)
            out_ref[t, h] = val.astype(BF16)
            return 0
        lax.fori_loop(0, heads, combine, 0)

    for copy in pending:
        copy.wait_send()

    def drain(c, _):
        for t in range(2):
            place = z if t == 0 else nz - 1 - z

            @pl.when(place < nz - 1)
            def _(t=t):
                chain_copy(t, c).wait_send()
        return 0
    lax.fori_loop(0, chunks, drain, 0)


PLAN = ((0, 0), (1, 0), (1, 0), (1, 0), (3, 6), (3, 6), (3, 6), (1, 4), (1, 4), (1, 3), (1, 3))


def run_state(q, k, v, g, decay, nz, nrow, nx):
    heads = nz * GH
    chunks = heads // HC
    cut = E // nrow
    half = nz // 2
    vm = pl.BlockSpec(memory_space=pltpu.VMEM)
    dma = pltpu.SemaphoreType.DMA
    return pl.pallas_call(
        functools.partial(state_kernel, nz, nrow, nx, PLAN),
        out_shape=(jax.ShapeDtypeStruct((2, heads, E, E), BF16),
                   jax.ShapeDtypeStruct((2, heads, E, E), BF16),
                   jax.ShapeDtypeStruct((heads, 2, E), F32)),
        in_specs=[vm] * 5,
        out_specs=(vm, vm, vm),
        scratch_shapes=[
            pltpu.VMEM((nz, 4 * GH, E), F32), pltpu.VMEM((nz, 4 * GH, E), F32),
            pltpu.VMEM((8, E), F32), pltpu.VMEM((nrow, 8, E), F32),
            pltpu.VMEM((8, E), F32), pltpu.VMEM((nx, 8, E), F32),
            pltpu.VMEM((nrow, 8, E), F32), pltpu.VMEM((nx, 8, E), F32),
            pltpu.VMEM((heads, 8, E), F32),
            pltpu.VMEM((2, heads, E, E), BF16),
            pltpu.VMEM((2, 2, half, GH, E, E), BF16),
            pltpu.VMEM((2, 2, half, GH, E, E), BF16),
            pltpu.VMEM((2, GH, E, E), BF16),
            pltpu.VMEM((nrow, 2, GH, cut, E), BF16),
            pltpu.VMEM((2, GH, cut, E), BF16),
            pltpu.VMEM((nx, 2, GH, cut, E), BF16),
            pltpu.VMEM((nrow, 2, GH, cut, E), BF16),
            pltpu.VMEM((nz, 2, GH, E, E), BF16),
            pltpu.VMEM((2, heads, E, E), BF16),
            pltpu.VMEM((2, heads, E, E), BF16),
            dma((nz - 1,)), dma, dma((nrow - 1,)), dma, dma((nx - 1,)), dma,
            dma((2, 2, half)), dma((2, 2, half)),
            dma((nrow - 1,)), dma,
            dma((nx - 1,)), dma,
            dma((nrow - 1,)), dma,
            dma((2, 2, half)), dma((2, 2, half)),
            dma((2, chunks)), dma((2, chunks)),
        ],
        compiler_params=pltpu.CompilerParams(collective_id=1, has_side_effects=True),
        name="state_scan",
    )(q, k, v, g, decay)


def output_kernel(heads, q_ref, k_ref, v_ref, g_ref, rc_ref, s_ref, sc_ref, a_ref, dq_ref, dk_ref, dv_ref):
    for i in range(heads):
        cols = pl.ds(i * E, E)
        q, k, v, g = q_ref[:, cols], k_ref[:, cols], v_ref[:, cols], g_ref[:, cols]
        r_col = column_of(rc_ref[i, 0:1, :])
        growth = SCALE * jnp.exp(-r_col)
        weight = jnp.exp(r_col - rc_ref[i, 1:2, :])
        scores, grads = sc_ref[0, i], sc_ref[1, i]
        state, back = s_ref[0, i], s_ref[1, i]
        a_ref[:, cols] = (dot(scores, v) + growth * dot(q, state)).astype(BF16)
        dq_ref[:, cols] = (dot(grads, k) + growth * ntdot(g, state)).astype(BF16)
        dk_ref[:, cols] = (tdot(grads, q) + weight * ntdot(v, back)).astype(BF16)
        dv_ref[:, cols] = (tdot(scores, g) + weight * dot(k, back)).astype(BF16)


def run_output(q, k, v, g, rc, states, scores, heads=4):
    n = rc.shape[0]
    tok = pl.BlockSpec((E, heads * E), lambda i: (0, i))
    mat = pl.BlockSpec((2, heads, E, E), lambda i: (0, i, 0, 0))
    return pl.pallas_call(
        functools.partial(output_kernel, heads),
        grid=(n // heads,),
        out_shape=(jax.ShapeDtypeStruct(q.shape, BF16),) * 4,
        in_specs=[tok, tok, tok, tok, pl.BlockSpec((heads, 2, E), lambda i: (i, 0, 0)), mat, mat],
        out_specs=(tok, tok, tok, tok),
        name="chunk_outputs",
    )(q, k, v, g, rc, states, scores)


def on_device(nz, nrow, nx, q, k, v, g, decay):
    states, scores, rc = run_state(q, k, v, g, decay, nz, nrow, nx)
    return run_output(q, k, v, g, rc, states, scores)


def solution(mesh):
    nz = mesh.shape["head"]
    nrow = ROWS
    nx = mesh.shape["seq"] // nrow
    tok = P(("seq", "head"), None)
    return jax.shard_map(
        functools.partial(on_device, nz, nrow, nx), mesh=mesh,
        in_specs=(tok, tok, tok, tok, P("head", "seq")),
        out_specs=(tok,) * 4, check_vma=False)
```

time: 139 us -> 116 us (0.83); the launches traced: 137 us -> 116 us
  Pallas kernels: 131 us -> 115 us
  other arithmetic: 4.79 us -> 0 us
    pallas_call x3 -> x1, Pallas kernels: 120 us -> 106 us  [run_state(): pl.pallas_call(functools.partial(state_kernel, nz, nrow, nx, PLAN), out_s...]
    exp x4 -> x0, other arithmetic: 4.79 us -> none  [the longest x1 1.47 us: on_device(): pre = jnp.exp(-start)]
    pallas_call x1, Pallas kernels: 11.7 us -> 9.11 us  [run_output(): pl.pallas_call(functools.partial(output_kernel, heads), grid=(n // heads,...]
where the time goes in v2:
time: 116 us
  Pallas kernels  115 us (99%)
    pallas_call x1, Pallas kernels, run_state(): pl.pallas_call(functools.partial(state_kernel, nz, nrow, nx, PLAN), out_s...  106 us
    pallas_call x1, Pallas kernels, run_output(): pl.pallas_call(functools.partial(output_kernel, heads), grid=(n // heads,...  9.11 us

profile of v2, /device:TPU:6, one launch (start us, length us, event | category | flops | bytes accessed | tf_op | source)
XLA Modules:
  0.0 116.1 jit_solution(208408965187289308)
XLA Ops:
  0.6 106.3 %state_scan.1 = (bf16[2,32,128,128]{3,2,1,0:T(8,128)(2,1)}, bf16[2,32,128,128]{3,2,1,0:T(8,128)(2,1)}, f32[32,2,128]{2,1,0:T(2,128)}) custom-call(bf16[128,4096]{1,0:T(8,128)(2,1)} %q_ref.3, bf16[128,4096]{1,0:T(8,128)(2,1)} %k_ref.3, bf16[128,4096]{1,0:T(8,128)(2,1)} %v_ref.3, bf16[128,4096]{1,0:T(8,128)(2,1)} %g_ref.3, f32[4,1024]{1,0:T(4,128)} %decay_ref.1), custom_call_target="tpu_custom_call" | custom-call | tf_op jit(solution)/shard_map/state_scan/pallas_call | solution.py:371
  106.9 9.1 %chunk_outputs.1 = (bf16[128,4096]{1,0:T(8,128)(2,1)}, bf16[128,4096]{1,0:T(8,128)(2,1)}, bf16[128,4096]{1,0:T(8,128)(2,1)}, bf16[128,4096]{1,0:T(8,128)(2,1)}) custom-call(bf16[128,4096]{1,0:T(8,128)(2,1)} %q_ref.3, bf16[128,4096]{1,0:T(8,128)(2,1)} %k_ref.3, bf16[128,4096]{1,0:T(8,128)(2,1)} %v_ref.3, bf16[128,4096]{1,0:T(8,128)(2,1)} %g_ref.3, ...), custom_call_target="tpu_custom_call" | custom-call | tf_op jit(solution)/shard_map/chunk_outputs/pallas_call | solution.py:427

commit v3 on v2

v3 whole, which is shorter than its diff:
```python
import functools

import jax
import jax.numpy as jnp
from jax import lax
from jax.experimental import pallas as pl
from jax.experimental.pallas import tpu as pltpu
from jax.sharding import PartitionSpec as P

E = 128
SCALE = E ** -0.5
GH = 4
HC = 2
LAG = 3
MIDDLE = 8
MESH = pl.DeviceIdType.MESH
F32 = jnp.float32
BF16 = jnp.bfloat16


def total_wait(ref, count, sem):
    part = ref.at[pl.ds(0, count)]
    pltpu.make_async_copy(part, part, sem).wait()


def barrier_with(peers):
    barrier = pltpu.get_barrier_semaphore()
    for peer in peers:
        pl.semaphore_signal(barrier, inc=1, device_id=peer, device_id_type=MESH)
    pl.semaphore_wait(barrier, len(peers))


def column_of(row):
    return jnp.transpose(jnp.broadcast_to(row, (E, E)))


def tdot(a, b):
    return lax.dot_general(a, b, (((0,), (0,)), ((), ())), preferred_element_type=F32)


def ntdot(a, b):
    return lax.dot_general(a, b, (((1,), (1,)), ((), ())), preferred_element_type=F32)


def dot(a, b):
    return jnp.dot(a, b, preferred_element_type=F32)


def state_kernel(nz, nseq, q_ref, k_ref, v_ref, g_ref, decay_ref,
                 out_ref, sc_ref, rc_ref,
                 msg, dz, bl, lb, eb, fac, u, tot, ta, so, sa, ch_in, ch_out,
                 dz_s, dz_r, lb_s, lb_r, tt_r, ta_s, ta_r, so_s, so_r, ag_s, ag_r, ch_s, ch_r):
    z = lax.axis_index("head")
    sq = lax.axis_index("seq")
    right = (z + 1) % nz
    left = (z + nz - 1) % nz
    heads = nz * GH
    chunks = heads // HC
    waves = chunks // nz
    members = nseq // 2
    cut = HC * E // members
    per = E // cut
    toward = ((sq, right), (sq, left))
    z_peers = [(z + i) % nz for i in range(1, nz)]
    s_peers = [(sq + i) % nseq for i in range(1, nseq)]
    barrier_with([(sq, p) for p in z_peers] + [(p, z) for p in s_peers])
    pending = []

    run = decay_ref[...]
    length = run.shape[1]
    lane = lax.broadcasted_iota(jnp.int32, run.shape, 1)
    shift = 1
    while shift < length:
        run = run + jnp.where(lane >= shift, pltpu.roll(run, shift, 1), 0.0)
        shift *= 2
    block_log = jnp.broadcast_to(run[:, length - 1:], (GH, E))
    start = jnp.zeros((GH, E), F32)
    for p in range(nz):
        part = run[:, p * E:(p + 1) * E]
        end = jnp.broadcast_to(part[:, E - 1:], (GH, E))
        msg[p, 0:GH, :] = part - start
        msg[p, GH:2 * GH, :] = start
        msg[p, 2 * GH:3 * GH, :] = block_log - end
        msg[p, 3 * GH:, :] = end - start
        start = end
    for i, p in enumerate(z_peers):
        pending.append(pltpu.make_async_remote_copy(
            msg.at[p], dz.at[z], dz_s.at[i], dz_r, device_id=(sq, p), device_id_type=MESH))
        pending[-1].start()
    dz[pl.ds(z, 1)] = msg[pl.ds(z, 1)]

    def hops(way, t):
        return nz // 2 if way == t else nz // 2 - 1

    def sign(way):
        return 1 if way == 0 else -1

    for t in range(2):
        place = z if t == 0 else nz - 1 - z

        @pl.when(place == 0)
        def _(t=t):
            def clear(h, _):
                ch_in[t, h] = jnp.zeros((E, E), BF16)
                return 0
            lax.fori_loop(0, heads, clear, 0)

    total_wait(dz, nz - 1, dz_r)
    for p in range(nz):
        for i in range(GH):
            start, rest, own = (dz[p, n * GH + i:n * GH + i + 1, :] for n in range(1, 4))
            rc_ref[p * GH + i, 0:1, :] = dz[p, i:i + 1, :]
            rc_ref[p * GH + i, 1:2, :] = own
            fac[p * GH + i, 0:1, :] = jnp.exp(-start)
            fac[p * GH + i, 1:2, :] = jnp.exp(-rest)
            fac[p * GH + i, 2:3, :] = jnp.exp(-own)
            fac[p * GH + i, 3:4, :] = start + rest + own

    def after(t, h):
        return fac[h, t:t + 1, :]

    def lb_copy(i):
        p = (sq + i) % nseq
        return pltpu.make_async_remote_copy(
            bl, lb.at[sq], lb_s.at[i], lb_r, device_id=(p, z), device_id_type=MESH)

    def send_logs():
        bl[...] = jnp.zeros((8, E), F32)
        for w in range(waves):
            for i in range(HC):
                bl[w * HC + i:w * HC + i + 1, :] = fac[(w * nz + z) * HC + i, 3:4, :]

        def one(i, _):
            lb_copy(i).start()
            return 0
        lax.fori_loop(1, nseq, one, 0)
        lb[pl.ds(sq, 1)] = bl[...][None]

    def fill(h):
        causal = (lax.broadcasted_iota(jnp.int32, (E, E), 0) >= lax.broadcasted_iota(jnp.int32, (E, E), 1))
        cols = pl.ds(pl.multiple_of(h * E, E), E)
        r_row = rc_ref[h, 0:1, :]
        r_col = column_of(r_row)
        mask = jnp.where(causal, jnp.exp(jnp.where(causal, r_row - r_col, 0.0)), 0.0) * SCALE
        sc_ref[0, h] = (ntdot(q_ref[:, cols], k_ref[:, cols]) * mask).astype(BF16)
        sc_ref[1, h] = (ntdot(g_ref[:, cols], v_ref[:, cols]) * mask).astype(BF16)

    def place_of(t):
        return z if t == 0 else nz - 1 - z

    def chain_copy(t, c):
        part = pl.ds(c * HC, HC)
        return pltpu.make_async_remote_copy(
            ch_out.at[t, part], ch_in.at[t, part], ch_s.at[t, c], ch_r.at[t, c],
            device_id=toward[t], device_id_type=MESH)

    def total_copy(t, c):
        w = c // nz
        return pltpu.make_async_remote_copy(
            ch_out.at[t, pl.ds(c * HC, HC)], tot.at[w, t], ch_s.at[t, c], tt_r.at[w, t],
            device_id=(sq, c % nz), device_id_type=MESH)

    def prepare(step):
        for t in range(2):
            c = step - LAG * place_of(t)

            @pl.when((c >= 0) & (c < chunks))
            def _(t=t, c=c):
                for i in range(HC):
                    h = c * HC + i
                    cols = pl.ds(pl.multiple_of(h * E, E), E)
                    r_col = column_of(rc_ref[h, 0:1, :])
                    if t == 0:
                        keyed = (k_ref[:, cols].astype(F32) * jnp.exp(r_col - rc_ref[h, 1:2, :])).astype(BF16)
                        u[step % 2, t, i] = tdot(keyed, v_ref[:, cols])
                    else:
                        queried = (q_ref[:, cols].astype(F32) * jnp.exp(-r_col)).astype(BF16)
                        u[step % 2, t, i] = SCALE * tdot(queried, g_ref[:, cols])

    def chain_step(step, _):
        for t in range(2):
            place = place_of(t)
            c = step - LAG * place

            @pl.when((c >= 0) & (c < chunks))
            def _(t=t, place=place, c=c):
                @pl.when(place > 0)
                def _():
                    chain_copy(t, c).wait_recv()
                for i in range(HC):
                    h = c * HC + i
                    ch_out[t, h] = (fac[h, 2:3, :] * ch_in[t, h].astype(F32) + u[step % 2, t, i]).astype(BF16)

                @pl.when(place < nz - 1)
                def _():
                    chain_copy(t, c).start()

                @pl.when((place == nz - 1) & (c % nz != z))
                def _():
                    total_copy(t, c).start()

                @pl.when((place == nz - 1) & (c % nz == z))
                def _():
                    tot[c // nz, t] = ch_out[t, pl.ds(c * HC, HC)]
        prepare(step + 1)

        @pl.when(step < heads)
        def _():
            fill(step)
        return 0

    chain_at = [0]
    chain_all = chunks + LAG * (nz - 1)

    def chain_run(count):
        count = min(count, chain_all - chain_at[0])
        if count > 0:
            lax.fori_loop(chain_at[0], chain_at[0] + count, chain_step, 0)
            chain_at[0] += count

    my_t = sq // members
    my_j = sq % members

    def rows_of(j):
        return pl.ds(pl.multiple_of((j % per) * cut, cut), cut)

    def ta_copy(w, t, j):
        p = t * members + j
        return pltpu.make_async_remote_copy(
            tot.at[w, t, j // per, rows_of(j), :], ta.at[w, sq], ta_s.at[w, p], ta_r.at[w],
            device_id=(p, z), device_id_type=MESH)

    def send_totals(w):
        for t in range(2):
            @pl.when(place_of(t) != nz - 1)
            def _(t=t):
                pltpu.make_async_remote_copy(
                    tot.at[w, t], tot.at[w, t], tt_r.at[w, t], tt_r.at[w, t],
                    device_id=toward[t], device_id_type=MESH).wait_recv()

            def send(j, _, t=t):
                @pl.when(t * members + j != sq)
                def _():
                    ta_copy(w, t, j).start()

                @pl.when(t * members + j == sq)
                def _():
                    ta[w, sq] = tot[w, t, j // per, rows_of(j), :]
                return 0
            lax.fori_loop(0, members, send, 0)

    def so_copy(w, p):
        return pltpu.make_async_remote_copy(
            so.at[w, p], sa.at[w, z, my_t, my_j // per, rows_of(my_j), :], so_s.at[w, p], so_r.at[w, my_t],
            device_id=(p, z), device_id_type=MESH)

    def scan_blocks(w):
        total_wait(ta.at[w], nseq - 1, ta_r.at[w])

        def one(n, acc):
            b = n + my_t * (nseq - 1 - 2 * n)
            so[w, b] = acc.astype(BF16)
            return eb[b, pl.ds(w * HC + my_j // per, 1), :] * acc + ta[w, b].astype(F32)
        lax.fori_loop(0, nseq, one, jnp.zeros((cut, E), F32), unroll=4)

        def send(i, _):
            so_copy(w, (sq + i) % nseq).start()
            return 0
        lax.fori_loop(1, nseq, send, 0)
        sa[w, z, my_t, my_j // per, rows_of(my_j), :] = so[w, sq]

    def so_wait(w, t):
        @pl.when(my_t == t)
        def _():
            total_wait(so.at[w], members - 1, so_r.at[w, t])

        @pl.when(my_t != t)
        def _():
            total_wait(so.at[w], members, so_r.at[w, t])

    def ag_copy(w, way, t, s):
        group = (z - sign(way) * s + nz) % nz
        return pltpu.make_async_remote_copy(
            sa.at[w, group, t], sa.at[w, group, t], ag_s.at[w, way, t, s], ag_r.at[w, way, t, s],
            device_id=toward[way], device_id_type=MESH)

    def ag_wait(w, way, t, s):
        group = (z - sign(way) * (s + 1) + 2 * nz) % nz
        pltpu.make_async_remote_copy(
            sa.at[w, group, t], sa.at[w, group, t], ag_s.at[w, way, t, s], ag_r.at[w, way, t, s],
            device_id=toward[way], device_id_type=MESH).wait_recv()

    def ag_hop(w, s):
        for t in range(2):
            if s == 0:
                so_wait(w, t)
            for way in range(2):
                if s >= hops(way, t):
                    continue
                if s > 0:
                    ag_wait(w, way, t, s - 1)
                pending.append(ag_copy(w, way, t, s))
                pending[-1].start()

    def combine(w, t, off):
        group = (z + off + nz) % nz
        for i in range(HC):
            h = (w * nz + group) * HC + i
            val = after(t, h) * sa[w, group, t, i].astype(F32) + ch_in[t, h].astype(F32)
            out_ref[t, h] = val.astype(BF16)

    def combine_early(w):
        for t in range(2):
            for off in range(t + 1 - nz // 2, nz // 2 - 1 + t):
                combine(w, t, off)

    def combine_last(w):
        for way, t in ((1, 0), (0, 1), (0, 0), (1, 1)):
            ag_wait(w, way, t, hops(way, t) - 1)
            combine(w, t, -sign(way) * hops(way, t))

    half = nz // 2
    prepare(0)
    chain_run(2)
    send_logs()
    chain_run(nz + LAG * (nz - 1) - 2)
    total_wait(lb, nseq - 1, lb_r)
    eb[...] = jnp.exp(-lb[...])
    send_totals(0)
    chain_run(MIDDLE)
    scan_blocks(0)
    chain_run(chain_all)
    send_totals(1)
    ag_hop(0, 0)
    if half > 2:
        ag_hop(0, 1)
    scan_blocks(1)
    for s in range(2, half - 1):
        ag_hop(0, s)
    ag_hop(1, 0)
    if half > 1:
        ag_hop(0, half - 1)
    combine_early(0)
    for s in range(1, half - 1):
        ag_hop(1, s)
    combine_last(0)
    if half > 1:
        ag_hop(1, half - 1)
    combine_early(1)
    combine_last(1)

    for copy in pending:
        copy.wait_send()

    def drain_peers(i, _):
        lb_copy(i).wait_send()
        for w in range(waves):
            so_copy(w, (sq + i) % nseq).wait_send()
        return 0
    lax.fori_loop(1, nseq, drain_peers, 0)

    def drain_totals(j, _):
        for w in range(waves):
            for t in range(2):
                @pl.when(t * members + j != sq)
                def _(w=w, t=t):
                    ta_copy(w, t, j).wait_send()
        return 0
    lax.fori_loop(0, members, drain_totals, 0)

    def drain_chain(c, _):
        for t in range(2):
            place = place_of(t)

            @pl.when((place < nz - 1) | (c % nz != z))
            def _(t=t):
                chain_copy(t, c).wait_send()
        return 0
    lax.fori_loop(0, chunks, drain_chain, 0)


def run_state(q, k, v, g, decay, nz, nseq):
    heads = nz * GH
    chunks = heads // HC
    waves = chunks // nz
    cut = 2 * HC * E // nseq
    half = nz // 2
    vm = pl.BlockSpec(memory_space=pltpu.VMEM)
    dma = pltpu.SemaphoreType.DMA
    return pl.pallas_call(
        functools.partial(state_kernel, nz, nseq),
        out_shape=(jax.ShapeDtypeStruct((2, heads, E, E), BF16),
                   jax.ShapeDtypeStruct((2, heads, E, E), BF16),
                   jax.ShapeDtypeStruct((heads, 2, E), F32)),
        in_specs=[vm] * 5,
        out_specs=(vm, vm, vm),
        scratch_shapes=[
            pltpu.VMEM((nz, 4 * GH, E), F32), pltpu.VMEM((nz, 4 * GH, E), F32),
            pltpu.VMEM((8, E), F32), pltpu.VMEM((nseq, 8, E), F32), pltpu.VMEM((nseq, 8, E), F32),
            pltpu.VMEM((heads, 8, E), F32),
            pltpu.VMEM((2, 2, HC, E, E), F32),
            pltpu.VMEM((waves, 2, HC, E, E), BF16),
            pltpu.VMEM((waves, nseq, cut, E), BF16),
            pltpu.VMEM((waves, nseq, cut, E), BF16),
            pltpu.VMEM((waves, nz, 2, HC, E, E), BF16),
            pltpu.VMEM((2, heads, E, E), BF16),
            pltpu.VMEM((2, heads, E, E), BF16),
            dma((nz - 1,)), dma, dma((nseq,)), dma, dma((waves, 2)),
            dma((waves, nseq)), dma((waves,)),
            dma((waves, nseq)), dma((waves, 2)),
            dma((waves, 2, 2, half)), dma((waves, 2, 2, half)),
            dma((2, chunks)), dma((2, chunks)),
        ],
        compiler_params=pltpu.CompilerParams(collective_id=1, has_side_effects=True),
        name="state_scan",
    )(q, k, v, g, decay)


def output_kernel(heads, q_ref, k_ref, v_ref, g_ref, rc_ref, s_ref, sc_ref, a_ref, dq_ref, dk_ref, dv_ref):
    for i in range(heads):
        cols = pl.ds(i * E, E)
        q, k, v, g = q_ref[:, cols], k_ref[:, cols], v_ref[:, cols], g_ref[:, cols]
        r_col = column_of(rc_ref[i, 0:1, :])
        growth = SCALE * jnp.exp(-r_col)
        weight = jnp.exp(r_col - rc_ref[i, 1:2, :])
        scores, grads = sc_ref[0, i], sc_ref[1, i]
        state, back = s_ref[0, i], s_ref[1, i]
        a_ref[:, cols] = (dot(scores, v) + growth * dot(q, state)).astype(BF16)
        dq_ref[:, cols] = (dot(grads, k) + growth * ntdot(g, state)).astype(BF16)
        dk_ref[:, cols] = (tdot(grads, q) + weight * ntdot(v, back)).astype(BF16)
        dv_ref[:, cols] = (tdot(scores, g) + weight * dot(k, back)).astype(BF16)


def run_output(q, k, v, g, rc, states, scores, heads=8):
    n = rc.shape[0]
    tok = pl.BlockSpec((E, heads * E), lambda i: (0, i))
    mat = pl.BlockSpec((2, heads, E, E), lambda i: (0, i, 0, 0))
    return pl.pallas_call(
        functools.partial(output_kernel, heads),
        grid=(n // heads,),
        out_shape=(jax.ShapeDtypeStruct(q.shape, BF16),) * 4,
        in_specs=[tok, tok, tok, tok, pl.BlockSpec((heads, 2, E), lambda i: (i, 0, 0)), mat, mat],
        out_specs=(tok, tok, tok, tok),
        name="chunk_outputs",
    )(q, k, v, g, rc, states, scores)


def on_device(nz, nseq, q, k, v, g, decay):
    states, scores, rc = run_state(q, k, v, g, decay, nz, nseq)
    return run_output(q, k, v, g, rc, states, scores)


def solution(mesh):
    nz = mesh.shape["head"]
    nseq = mesh.shape["seq"]
    tok = P(("seq", "head"), None)
    return jax.shard_map(
        functools.partial(on_device, nz, nseq), mesh=mesh,
        in_specs=(tok, tok, tok, tok, P("head", "seq")),
        out_specs=(tok,) * 4, check_vma=False)
```

time: 116 us -> 109 us (0.940)
  Pallas kernels: 115 us -> 109 us
    pallas_call x1, Pallas kernels: 106 us -> 101 us  [run_state(): pl.pallas_call(functools.partial(state_kernel, nz, nseq), out_shape=(jax....]
    pallas_call x1, Pallas kernels: 9.11 us -> 7.24 us  [run_output(): pl.pallas_call(functools.partial(output_kernel, heads), grid=(n // heads,...]
where the time goes in v3:
time: 109 us
  Pallas kernels  109 us (100%)
    pallas_call x1, Pallas kernels, run_state(): pl.pallas_call(functools.partial(state_kernel, nz, nseq), out_shape=(jax....  101 us
    pallas_call x1, Pallas kernels, run_output(): pl.pallas_call(functools.partial(output_kernel, heads), grid=(n // heads,...  7.24 us

profile of v3, /device:TPU:6, one launch (start us, length us, event | category | flops | bytes accessed | tf_op | source)
XLA Modules:
  0.0 109.2 jit_solution(7656099743044783861)
XLA Ops:
  0.6 101.3 %state_scan.1 = (bf16[2,32,128,128]{3,2,1,0:T(8,128)(2,1)}, bf16[2,32,128,128]{3,2,1,0:T(8,128)(2,1)}, f32[32,2,128]{2,1,0:T(2,128)}) custom-call(bf16[128,4096]{1,0:T(8,128)(2,1)} %q_ref.3, bf16[128,4096]{1,0:T(8,128)(2,1)} %k_ref.3, bf16[128,4096]{1,0:T(8,128)(2,1)} %v_ref.3, bf16[128,4096]{1,0:T(8,128)(2,1)} %g_ref.3, f32[4,1024]{1,0:T(4,128)} %decay_ref.1), custom_call_target="tpu_custom_call" | custom-call | tf_op jit(solution)/shard_map/state_scan/pallas_call | solution.py:390
  101.9 7.2 %chunk_outputs.1 = (bf16[128,4096]{1,0:T(8,128)(2,1)}, bf16[128,4096]{1,0:T(8,128)(2,1)}, bf16[128,4096]{1,0:T(8,128)(2,1)}, bf16[128,4096]{1,0:T(8,128)(2,1)}) custom-call(bf16[128,4096]{1,0:T(8,128)(2,1)} %q_ref.3, bf16[128,4096]{1,0:T(8,128)(2,1)} %k_ref.3, bf16[128,4096]{1,0:T(8,128)(2,1)} %v_ref.3, bf16[128,4096]{1,0:T(8,128)(2,1)} %g_ref.3, ...), custom_call_target="tpu_custom_call" | custom-call | tf_op jit(solution)/shard_map/chunk_outputs/pallas_call | solution.py:438

commit v4 on v3

--- a/solution.py
+++ b/solution.py
@@ -340,12 +340,12 @@
     ag_hop(1, 0)
     if half > 1:
         ag_hop(0, half - 1)
-    combine_early(0)
     for s in range(1, half - 1):
         ag_hop(1, s)
-    combine_last(0)
+        combine_early(0) if s == 1 else None
     if half > 1:
         ag_hop(1, half - 1)
+    combine_last(0)
     combine_early(1)
     combine_last(1)
 

time: 109 us -> 109 us (level)
  no operation moved by 1% of the time
where the time goes in v4:
time: 109 us
  Pallas kernels  109 us (100%)
    pallas_call x1, Pallas kernels, run_state(): pl.pallas_call(functools.partial(state_kernel, nz, nseq), out_shape=(jax....  101 us
    pallas_call x1, Pallas kernels, run_output(): pl.pallas_call(functools.partial(output_kernel, heads), grid=(n // heads,...  7.24 us

profile of v4, /device:TPU:6, one launch (start us, length us, event | category | flops | bytes accessed | tf_op | source)
XLA Modules:
  0.0 109.2 jit_solution(16539597021040067646)
XLA Ops:
  0.6 101.3 %state_scan.1 = (bf16[2,32,128,128]{3,2,1,0:T(8,128)(2,1)}, bf16[2,32,128,128]{3,2,1,0:T(8,128)(2,1)}, f32[32,2,128]{2,1,0:T(2,128)}) custom-call(bf16[128,4096]{1,0:T(8,128)(2,1)} %q_ref.3, bf16[128,4096]{1,0:T(8,128)(2,1)} %k_ref.3, bf16[128,4096]{1,0:T(8,128)(2,1)} %v_ref.3, bf16[128,4096]{1,0:T(8,128)(2,1)} %g_ref.3, f32[4,1024]{1,0:T(4,128)} %decay_ref.1), custom_call_target="tpu_custom_call" | custom-call | tf_op jit(solution)/shard_map/state_scan/pallas_call | solution.py:390
  101.9 7.2 %chunk_outputs.1 = (bf16[128,4096]{1,0:T(8,128)(2,1)}, bf16[128,4096]{1,0:T(8,128)(2,1)}, bf16[128,4096]{1,0:T(8,128)(2,1)}, bf16[128,4096]{1,0:T(8,128)(2,1)}) custom-call(bf16[128,4096]{1,0:T(8,128)(2,1)} %q_ref.3, bf16[128,4096]{1,0:T(8,128)(2,1)} %k_ref.3, bf16[128,4096]{1,0:T(8,128)(2,1)} %v_ref.3, bf16[128,4096]{1,0:T(8,128)(2,1)} %g_ref.3, ...), custom_call_target="tpu_custom_call" | custom-call | tf_op jit(solution)/shard_map/chunk_outputs/pallas_call | solution.py:438
